TPU v7x, 128 devices: a whole 4x4x4 slice. The times are simulated.
128 devices in a mesh: batch: 4 (over y_hi, core), tm: 8 (over x, y_lo), space: 4 (over z).
Axes of the slice: x: 4, y: 4 (y_hi: 2, y_lo: 2; y = y_hi * 2 + y_lo), z: 4, core: 2. Of those that a mesh axis runs over, the one named last changes fastest.
Arguments:
- clip_tokens: bfloat16 [4, 16, 32, 32, 1024], P('batch', None, 'space', 'tm'), may hold values from -6 to 6
- frame_order: int32 [4, 16], P('batch'), may hold values from 0 to 15, each once within a row
- row_reach: int32 [4, 16], P('batch', 'tm'), may hold values from 1 to 4
- spatial_gain: float32 [1024], replicated, may hold values from 0.1 to 1.9
- spatial_heads: bfloat16 [1024, 3072], replicated, may hold values from -2 to 2
- spatial_merge: bfloat16 [1024, 1024], replicated, may hold values from -0.1875 to 0.1875
- temporal_gain: float32 [1024], replicated, may hold values from 0.1 to 1.9
- temporal_heads: bfloat16 [1024, 3072], replicated, may hold values from -2 to 2
- temporal_merge: bfloat16 [1024, 1024], replicated, may hold values from -0.1875 to 0.1875
- cotangent: bfloat16 [4, 16, 32, 32, 1024], P('batch', 'tm', 'space'), may hold values from -0.059814453 to 0.059814453
Outputs:
- output: bfloat16 [4, 16, 32, 32, 1024], P('batch', 'tm', 'space')
- weight_grad: float32 [1024, 1024], P(('tm', 'space'))
Inputs may be any that keep to these rules, and one draw needn't show every extreme that they name: Each row of frame_order names every number from 0 to 15 once.
All inputs are finite; a program needn't handle non-finite values.
Results may differ from a plain program's by a relative error of at most 0.025.
Values may be sent and summed in bfloat16 or wider, within the bound.
A program may use at most 128 MiB of HBM per device.

v0:
```python
import jax
import jax.numpy as jnp
from jax import lax
from jax.sharding import PartitionSpec as P

HALO = 4
D = 1024
HEADS = 16
HEAD_DIM = 64


floor_term = 0.5


def extended(value, sides, width):
    for axis, dim in sides:
        devices, length = (lax.axis_size(axis), value.shape[dim])
        up = [(i, (i + 1) % devices) for i in range(devices - 1)]
        down = [(j, i) for i, j in up]
        last = lax.slice_in_dim(value, length - width, length, axis=dim)
        initial = lax.slice_in_dim(value, 0, width, axis=dim)
        before = lax.ppermute(last, axis, up)
        after = lax.ppermute(initial, axis, down)
        value = jnp.concatenate([before, value, after], axis=dim)
    return value


def in_blocks(value, dim, devices):
    before, after = (value.shape[:dim], value.shape[dim + 1 :])
    return jnp.moveaxis(value.reshape(*before, devices, -1, *after), dim, 0)


def summed_on_arrival(value, axis, dim):
    parts = in_blocks(value, dim, lax.axis_size(axis))
    arrived = lax.all_to_all(parts, axis, split_axis=0, concat_axis=0, tiled=True)
    return arrived.astype(jnp.float32).sum(axis=0)


def gathered_total(value, axis):
    return lax.all_gather(value, axis).astype(jnp.float32).sum(0)


def normalize(values, gain_vector):
    widened = values.astype(jnp.float32)
    scaled = widened * lax.rsqrt(jnp.mean(widened * widened, axis=-1, keepdims=True) + floor_term)
    return (scaled * gain_vector).astype(jnp.bfloat16)


def softmax_rounded(scores, allowed):
    masked = jnp.where(allowed, scores, -1e30)
    top_score = jnp.max(masked, axis=-1, keepdims=True)
    exponent = jnp.exp(masked - top_score)
    return (exponent / jnp.sum(exponent, axis=-1, keepdims=True)).astype(jnp.bfloat16)


def temporal_attend(queries, keys_all, values_all, query_order, key_order):
    clip_count, query_frames, positions, _ = queries.shape
    key_frames = keys_all.shape[1]
    query_heads = queries.reshape(clip_count, query_frames, positions, HEADS, HEAD_DIM)
    key_heads = keys_all.reshape(clip_count, key_frames, positions, HEADS, HEAD_DIM)
    value_heads = values_all.reshape(clip_count, key_frames, positions, HEADS, HEAD_DIM)
    scores = jnp.einsum(
        "cfthd,cgthd->cthfg", query_heads, key_heads, preferred_element_type=jnp.float32
    ) * HEAD_DIM ** (-0.5)
    allowed = key_order[:, None, :] <= query_order[:, :, None]
    weights = softmax_rounded(scores, allowed[:, None, None])
    context = jnp.einsum(
        "cthfg,cgthd->cfthd", weights, value_heads, preferred_element_type=jnp.float32
    )
    return context.reshape(clip_count, query_frames, positions, D).astype(jnp.bfloat16)


def per_device(
    clip_tokens,
    frame_order,
    row_reach,
    spatial_gain,
    spatial_heads,
    spatial_merge,
    temporal_gain,
    temporal_heads,
    temporal_merge,
    cotangent,
):
    frames_here = lax.all_to_all(clip_tokens, "tm", split_axis=1, concat_axis=3, tiled=True)
    clip_count, frame_count, row_count, col_count, _ = frames_here.shape
    tokens = row_count * col_count
    normed = normalize(frames_here, spatial_gain)
    projected = jnp.dot(normed, spatial_heads, preferred_element_type=jnp.float32).astype(
        jnp.bfloat16
    )
    widened = extended(normed, (("space", 2),), HALO)
    key_weight = spatial_heads[:, D:]
    upper_rows = jnp.dot(
        widened[:, :, :HALO], key_weight, preferred_element_type=jnp.float32
    ).astype(jnp.bfloat16)
    lower_rows = jnp.dot(
        widened[:, :, HALO + row_count :], key_weight, preferred_element_type=jnp.float32
    ).astype(jnp.bfloat16)
    key_value = jnp.concatenate([upper_rows, projected[..., D:], lower_rows], axis=2)
    extent = (row_count + 2 * HALO) * col_count
    first_row = lax.axis_index("space") * row_count
    all_rows = row_count * lax.axis_size("space")
    query_rows = first_row + jnp.arange(tokens, dtype=jnp.int32) // col_count
    key_rows = first_row - HALO + jnp.arange(extent, dtype=jnp.int32) // col_count
    inside = (key_rows >= 0) & (key_rows < all_rows)
    distance = jnp.abs(key_rows[None, :] - query_rows[:, None])

    def spatial_item(inputs):
        queries, key_pairs, reach_now = inputs
        query_heads = queries.reshape(tokens, HEADS, HEAD_DIM)
        key_heads = key_pairs[:, :D].reshape(extent, HEADS, HEAD_DIM)
        value_heads = key_pairs[:, D:].reshape(extent, HEADS, HEAD_DIM)
        scores = jnp.einsum(
            "qhd,khd->hqk", query_heads, key_heads, preferred_element_type=jnp.float32
        ) * HEAD_DIM ** (-0.5)
        allowed = inside[None, :] & (distance <= reach_now)
        weights = softmax_rounded(scores, allowed[None])
        context = jnp.einsum(
            "hqk,khd->qhd", weights, value_heads, preferred_element_type=jnp.float32
        )
        return context.reshape(tokens, D).astype(jnp.bfloat16)

    item_count = clip_count * frame_count
    spatial_context = lax.map(
        spatial_item,
        (
            projected[..., :D].reshape(item_count, tokens, D),
            key_value.reshape(item_count, extent, 2 * D),
            row_reach.reshape(item_count),
        ),
    )
    flat_input = frames_here.reshape(clip_count, frame_count, tokens, D)
    spatial_context = spatial_context.reshape(clip_count, frame_count, tokens, D)
    middle = (
        flat_input.astype(jnp.float32)
        + jnp.dot(spatial_context, spatial_merge, preferred_element_type=jnp.float32)
    ).astype(jnp.bfloat16)
    normed_two = normalize(middle, temporal_gain)
    projected_two = jnp.dot(normed_two, temporal_heads, preferred_element_type=jnp.float32).astype(
        jnp.bfloat16
    )
    regrouped = lax.all_to_all(projected_two, "tm", split_axis=2, concat_axis=1, tiled=True)
    context_all = temporal_attend(
        regrouped[..., :D],
        regrouped[..., D : 2 * D],
        regrouped[..., 2 * D :],
        frame_order,
        frame_order,
    )
    temporal_context = lax.all_to_all(context_all, "tm", split_axis=1, concat_axis=2, tiled=True)
    output = (
        middle.astype(jnp.float32)
        + jnp.dot(temporal_context, temporal_merge, preferred_element_type=jnp.float32)
    ).astype(jnp.bfloat16)
    flat_context = temporal_context.reshape(-1, D)
    flat_cotangent = cotangent.reshape(-1, D)
    own_rows = summed_on_arrival(
        lax.dot_general(
            flat_context,
            flat_cotangent,
            (((0,), (0,)), ((), ())),
            preferred_element_type=jnp.float32,
        ).astype(jnp.bfloat16),
        ("tm", "space"),
        0,
    )
    weight_grad = gathered_total(own_rows.astype(jnp.bfloat16), "batch").astype(jnp.float32)
    return (output.reshape(clip_count, frame_count, row_count, col_count, D), weight_grad)


def solution(mesh):
    in_specs = (
        P("batch", None, "space", "tm", None),
        P("batch", None),
        P("batch", "tm"),
        P(),
        P(),
        P(),
        P(),
        P(),
        P(),
        P("batch", "tm", "space", None, None),
    )
    out_specs = (P("batch", "tm", "space", None, None), P(("tm", "space"), None))
    return jax.shard_map(
        per_device, mesh=mesh, in_specs=in_specs, out_specs=out_specs, check_vma=False
    )
```

profile of v0, /device:TPU:1, one launch (start us, length us, event | category | flops | bytes accessed | tf_op | source)
XLA Modules:
  0.0 272.9 jit_solution(8427147431864572981)
XLA Ops:
  0.6 6.0 %all-to-all-start = ((bf16[1,16,8,4,1024]{4,3,2,0,1:T(4,128)(2,1)}), bf16[1,16,8,4,1024]{4,3,2,0,1:T(4,128)(2,1)S(1)}, u32[]{:S(2)}, u32[]{:S(2)}) async-start(bf16[1,16,8,4,1024]{4,3,2,0,1:T(4,128)(2,1)} %bitcast.156), calls=%async_computation | async-start | bytes 2097152 | tf_op jit(solution)/shard_map/all_to_all | solution.py:85
  6.7 15.3 %all-to-all-done = bf16[1,16,8,4,1024]{4,3,2,0,1:T(4,128)(2,1)S(1)} async-done(((bf16[1,16,8,4,1024]{4,3,2,0,1:T(4,128)(2,1)}), bf16[1,16,8,4,1024]{4,3,2,0,1:T(4,128)(2,1)S(1)}, u32[]{:S(2)}, u32[]{:S(2)}) %all-to-all-start) | async-done | bytes 1048608 | tf_op jit(solution)/shard_map/all_to_all | solution.py:85
  21.9 2.0 copy_bitcast_fusion
  23.9 3.0 %reshape.333 = f32[2,8,32,1024]{3,2,1,0:T(8,128)} reshape(f32[1,2,8,8,4,1024]{5,4,3,2,1,0:T(4,128)} %copy_bitcast_fusion) | data formatting | bytes 4194304 | tf_op jit(solution)/shard_map/convert_element_type | solution.py:44
  26.9 3.0 %reshape.330 = f32[1,2,8,32,1024]{4,3,2,1,0:T(8,128)} reshape(f32[1,2,8,8,4,1024]{5,4,3,2,1,0:T(4,128)} %copy_bitcast_fusion) | data formatting | bytes 4194304 | tf_op jit(solution)/shard_map/convert_element_type | solution.py:44
  30.8 2.0 multiply_convert_fusion.1
  32.9 1.3 collective-permute-start.1
  34.2 5.0 %collective-permute-start = (bf16[1,2,4,32,1024]{4,3,2,1,0:T(8,128)(2,1)S(1)}, bf16[1,2,4,32,1024]{4,3,2,1,0:T(8,128)(2,1)}, u32[]{:S(2)}, u32[]{:S(2)}) collective-permute-start(bf16[1,2,4,32,1024]{4,3,2,1,0:T(8,128)(2,1)S(1)} %get-tuple-element.133), channel_id=1, source_target_pairs={{0,1},{1,2},{2,3},{4,5},{5,6},{6,7},{8,9},{9,10},{10,11},{12,13},{... | collective-permute-start | bytes 1572872 | tf_op jit(solution)/shard_map/ppermute | solution.py:22
  39.1 6.5 %fusion.35 = bf16[1,2,8,32,3072]{4,3,2,1,0:T(8,128)(2,1)S(1)} fusion(bf16[1024,3072]{1,0:T(8,128)(2,1)} %param.16, f32[2,8,32,1024]{3,2,1,0:T(8,128)S(1)} %copy-done.7, f32[1024]{0:T(1024)S(1)} %copy-done.8, f32[2,8,32]{2,1,0:T(8,128)S(1)} %copy.95), kind=kOutput, calls=%fused_computation.45 | convolution fusion | flops 3224371200 | bytes 11540480 | tf_op jit(solution)/shard_map/dot_general | solution.py:89
  45.7 1.6 copy-done.3
  47.3 1.1 slice.45
  48.4 2.9 %reshape.329 = f32[2,256,1024]{2,1,0:T(8,128)} reshape(f32[1,2,8,8,4,1024]{5,4,3,2,1,0:T(4,128)} %copy_bitcast_fusion) | data formatting | bytes 4194304 | tf_op jit(solution)/shard_map/convert_element_type | solution.py:136
  51.4 3.6 %fusion.50 = bf16[1,2,4,32,2048]{4,3,2,1,0:T(8,128)(2,1)S(1)} fusion(bf16[1024,3072]{1,0:T(8,128)(2,1)} %param.16, bf16[1,2,4,32,1024]{4,3,2,1,0:T(8,128)(2,1)} %collective-permute-done.1), kind=kOutput, calls=%fused_computation.55 | convolution fusion | flops 1074266112 | bytes 5767168 | tf_op jit(solution)/shard_map/dot_general | solution.py:97
  55.0 3.7 %fusion.53 = bf16[1,2,4,32,2048]{4,3,2,1,0:T(8,128)(2,1)S(1)} fusion(bf16[1024,3072]{1,0:T(8,128)(2,1)} %param.16, bf16[1,2,4,32,1024]{4,3,2,1,0:T(8,128)(2,1)} %collective-permute-done), kind=kOutput, calls=%fused_computation.56 | convolution fusion | flops 1074266112 | bytes 5767168 | tf_op jit(solution)/shard_map/dot_general | solution.py:94
  58.8 2.2 pad_maximum_fusion
  61.0 52.2 %while.11 = (s32[]{:T(128)}, bf16[2,256,1024]{1,2,0:T(8,128)(2,1)}, bf16[2,512,2048]{2,1,0:T(8,128)(2,1)}, s32[2]{0:T(128)S(1)}, bf16[2,256,1024]{2,1,0:T(8,128)...) while((s32[]{:T(128)}, bf16[2,256,1024]{1,2,0:T(8,128)(2,1)}, ...), condition=%wide.region_4.5_spmd.clone, body=%wide.region_1.4_spmd.clone.sunk | while | flops 550246912 | bytes 44339888 | solution.py:125
  62.6 3.2 %constant_dynamic-slice_fusion.4 = bf16[1,512,2048]{2,1,0:T(8,128)(2,1)} fusion(bf16[2,512,2048]{2,1,0:T(8,128)(2,1)} %get-tuple-element.216, s32[]{:T(128)} %get-tuple-element.205), kind=kLoop, calls=%fused_computation.26.clone.1 | loop fusion | bytes 4194308 | tf_op jit(solution)/shard_map/while/body/jit(dynamic_index_in_dim)/dynamic_slice | solution.py:125
  65.8 3.9 %copy.132 = bf16[1,512,2048]{1,2,0:T(8,128)(2,1)} copy(bf16[1,512,2048]{2,1,0:T(8,128)(2,1)} %constant_dynamic-slice_fusion.4) | data formatting | bytes 4194304 | tf_op jit(solution)/shard_map/while/body/jit(dynamic_index_in_dim)/dynamic_slice | solution.py:125
  69.7 3.1 %fusion.119 = (bf16[512,1024]{0,1:T(8,128)(2,1)}, bf16[512,1024]{0,1:T(8,128)(2,1)}) fusion(bf16[512,2048]{0,1:T(8,128)(2,1)} %bitcast.141), kind=kLoop, calls=%fused_computation.108.clone.1 | loop fusion | bytes 4194304 | tf_op jit(solution)/shard_map/while/body/eval_jaxpr/slice | solution.py:112
  73.8 7.6 %fusion.121 = (f32[16,256]{1,0:T(8,128)S(1)}, f32[16,256,512]{2,1,0:T(8,128)}) fusion(pred[256,512]{1,0:T(8,128)(4,1)S(1)} %fusion.120, bf16[256,16,64]{0,2,1:T(8,128)(2,1)} %bitcast.145, bf16[512,16,64]{0,2,1:T(8,128)(2,1)} %bitcast.144), kind=kOutput, calls=%fused_computation.109.clone.1 | convolution fusion | flops 276824576 | bytes 10108928 | tf_op jit(solution)/shard_map/while/body/eval_jaxpr/sub | solution.py:52
  81.4 4.9 %fusion.122 = bf16[16,64,256]{2,1,0:T(8,128)(2,1)S(1)} fusion(bf16[512,16,64]{0,2,1:T(8,128)(2,1)S(1)} %bitcast.143, f32[16,256,512]{2,1,0:T(8,128)} %get-tuple-element.194, f32[16,256]{1,0:T(8,128)S(1)} %get-tuple-element.195), kind=kOutput, calls=%fused_computation.11.clone.1 | convolution fusion | flops 272891904 | bytes 9977856 | tf_op jit(solution)/shard_map/while/body/eval_jaxpr/hqk,khd->qhd/dot_general | solution.py:119
  88.7 3.2 %constant_dynamic-slice_fusion.4 = bf16[1,512,2048]{2,1,0:T(8,128)(2,1)} fusion(bf16[2,512,2048]{2,1,0:T(8,128)(2,1)} %get-tuple-element.216, s32[]{:T(128)} %get-tuple-element.205), kind=kLoop, calls=%fused_computation.26.clone.1 | loop fusion | bytes 4194308 | tf_op jit(solution)/shard_map/while/body/jit(dynamic_index_in_dim)/dynamic_slice | solution.py:125
  91.9 3.9 %copy.132 = bf16[1,512,2048]{1,2,0:T(8,128)(2,1)} copy(bf16[1,512,2048]{2,1,0:T(8,128)(2,1)} %constant_dynamic-slice_fusion.4) | data formatting | bytes 4194304 | tf_op jit(solution)/shard_map/while/body/jit(dynamic_index_in_dim)/dynamic_slice | solution.py:125
  95.8 3.1 %fusion.119 = (bf16[512,1024]{0,1:T(8,128)(2,1)}, bf16[512,1024]{0,1:T(8,128)(2,1)}) fusion(bf16[512,2048]{0,1:T(8,128)(2,1)} %bitcast.141), kind=kLoop, calls=%fused_computation.108.clone.1 | loop fusion | bytes 4194304 | tf_op jit(solution)/shard_map/while/body/eval_jaxpr/slice | solution.py:112
  99.9 7.6 %fusion.121 = (f32[16,256]{1,0:T(8,128)S(1)}, f32[16,256,512]{2,1,0:T(8,128)}) fusion(pred[256,512]{1,0:T(8,128)(4,1)S(1)} %fusion.120, bf16[256,16,64]{0,2,1:T(8,128)(2,1)} %bitcast.145, bf16[512,16,64]{0,2,1:T(8,128)(2,1)} %bitcast.144), kind=kOutput, calls=%fused_computation.109.clone.1 | convolution fusion | flops 276824576 | bytes 10108928 | tf_op jit(solution)/shard_map/while/body/eval_jaxpr/sub | solution.py:52
  107.6 4.9 %fusion.122 = bf16[16,64,256]{2,1,0:T(8,128)(2,1)S(1)} fusion(bf16[512,16,64]{0,2,1:T(8,128)(2,1)S(1)} %bitcast.143, f32[16,256,512]{2,1,0:T(8,128)} %get-tuple-element.194, f32[16,256]{1,0:T(8,128)S(1)} %get-tuple-element.195), kind=kOutput, calls=%fused_computation.11.clone.1 | convolution fusion | flops 272891904 | bytes 9977856 | tf_op jit(solution)/shard_map/while/body/eval_jaxpr/hqk,khd->qhd/dot_general | solution.py:119
  113.3 3.3 %fusion.56 = (f32[2,256]{1,0:T(2,128)S(1)}, bf16[2,256,1024]{2,1,0:T(8,128)(2,1)S(1)}) fusion(f32[2,256,1024]{2,1,0:T(8,128)} %reshape.329, bf16[2,256,1024]{1,2,0:T(8,128)(2,1)} %get-tuple-element.39, bf16[1024,1024]{1,0:T(8,128)(2,1)S(1)} %copy-done), kind=kOutput, calls=%fused_computation.57 | convolution fusion | flops 1076362752 | bytes 6293504 | tf_op jit(solution)/shard_map/dot_general | solution.py:137
  117.5 6.6 %fusion.38 = bf16[1,2,256,3072]{3,2,1,0:T(8,128)(2,1)S(1)} fusion(bf16[1024,3072]{1,0:T(8,128)(2,1)} %param.19, bf16[2,256,1024]{2,1,0:T(8,128)(2,1)S(1)} %get-tuple-element.136, f32[1024]{0:T(1024)S(1)} %copy-done.10, f32[2,256]{1,0:T(2,128)S(1)} %add_rsqrt_fusion.1), kind=kOutput, calls=%fused_computation.46 | convolution fusion | flops 3224895488 | bytes 10491904 | tf_op jit(solution)/shard_map/dot_general | solution.py:140
  124.1 4.9 %copy.100 = bf16[1,2,256,3072]{3,1,0,2:T(2,128)(2,1)} copy(bf16[1,2,256,3072]{3,2,1,0:T(8,128)(2,1)S(1)} %fusion.38) | data formatting | bytes 6291456 | tf_op jit(solution)/shard_map/convert_element_type | solution.py:140
  129.0 4.6 %all-to-all-start.1 = ((bf16[1,2,256,3072]{3,1,0,2:T(2,128)(2,1)}), bf16[1,2,256,3072]{3,1,0,2:T(2,128)(2,1)}, u32[]{:S(2)}, u32[]{:S(2)}) async-start(bf16[1,2,256,3072]{3,1,0,2:T(2,128)(2,1)} %copy.100), calls=%async_computation.1 | async-start | bytes 6291456 | tf_op jit(solution)/shard_map/all_to_all | solution.py:143
  133.7 44.3 %all-to-all-done.1 = bf16[1,2,256,3072]{3,1,0,2:T(2,128)(2,1)} async-done(((bf16[1,2,256,3072]{3,1,0,2:T(2,128)(2,1)}), bf16[1,2,256,3072]{3,1,0,2:T(2,128)(2,1)}, u32[]{:S(2)}, u32[]{:S(2)}) %all-to-all-start.1) | async-done | bytes 3145760 | tf_op jit(solution)/shard_map/all_to_all | solution.py:143
  178.0 2.7 copy.101
  181.0 1.7 fusion.98
  182.7 4.0 %reshape.322 = bf16[16,32,16,64]{3,2,1,0:T(8,128)(2,1)} reshape(bf16[1,16,32,1024]{3,2,1,0:T(8,128)(2,1)} %get-tuple-element.132) | data formatting | bytes 2097152 | tf_op jit(solution)/shard_map/reshape.38
  186.7 4.0 %reshape.323 = bf16[16,32,16,64]{3,2,1,0:T(8,128)(2,1)} reshape(bf16[1,16,32,1024]{3,2,1,0:T(8,128)(2,1)} %get-tuple-element.131) | data formatting | bytes 2097152 | tf_op jit(solution)/shard_map/reshape.39
  190.7 2.3 reshape.321
  193.1 4.7 %fusion.66 = f32[32,16,16,16]{2,3,1,0:T(8,128)S(1)} fusion(bf16[16,32,16,64]{3,2,1,0:T(8,128)(2,1)} %reshape.323, bf16[16,32,16,64]{3,2,1,0:T(8,128)(2,1)} %reshape.322), kind=kOutput, calls=%fused_computation.68 | convolution fusion | flops 16777216 | bytes 2621440 | tf_op jit(solution)/shard_map/cfthd,cgthd->cthfg/dot_general | solution.py:62
  197.8 2.0 fusion.100
  199.8 1.7 convert_bitcast_fusion
  201.5 1.9 copy.107
  203.4 3.2 %convert_element_type.175 = bf16[1,16,32,1024]{3,2,1,0:T(8,128)(2,1)S(1)} reshape(bf16[1,16,32,16,64]{4,3,2,1,0:T(8,128)(2,1)} %copy.107) | data formatting | bytes 2097152 | tf_op jit(solution)/shard_map/convert_element_type | solution.py:70
  206.7 15.3 %all_to_all.47 = bf16[1,16,32,1024]{3,2,0,1:T(8,128)(2,1)S(1)} all-to-all(bf16[1,16,32,1024]{3,2,0,1:T(8,128)(2,1)S(1)} %bitcast.151), channel_id=1, replica_groups=mesh['batch'=4,'tm'=8,'space'=4] {'tm'}, dimensions={1} | all-to-all | bytes 2097152 | tf_op jit(solution)/shard_map/all_to_all | solution.py:151
  221.9 4.2 %bitcast_convert_fusion = bf16[1024,1024]{1,0:T(8,128)(2,1)} fusion(bf16[1,2,8,32,1024]{4,3,2,1,0:T(8,128)(2,1)} %param.21, bf16[1,8,2,32,1024]{4,3,2,1,0:T(8,128)(2,1)S(1)} %bitcast.152), kind=kOutput, calls=%fused_computation.37 | convolution fusion | flops 1074790400 | bytes 4194304 | tf_op jit(solution)/shard_map/dot_general | solution.py:159
  226.2 7.3 %all-to-all-start.3 = ((bf16[32,32,1024]{2,1,0:T(8,128)(2,1)}), bf16[32,32,1024]{2,1,0:T(8,128)(2,1)}, u32[]{:S(2)}, u32[]{:S(2)}) async-start(bf16[32,32,1024]{2,1,0:T(8,128)(2,1)} %bitcast.154), calls=%async_computation.3 | async-start | bytes 4194304 | tf_op jit(solution)/shard_map/all_to_all | solution.py:35
  233.6 4.1 %fusion.59 = bf16[2,256,1024]{2,1,0:T(8,128)(2,1)} fusion(bf16[2,256,1024]{2,1,0:T(8,128)(2,1)} %copy-done.12, bf16[2,256,1024]{2,1,0:T(8,128)(2,1)S(1)} %bitcast.157, bf16[1024,1024]{1,0:T(8,128)(2,1)} %param.20), kind=kOutput, calls=%fused_computation.60 | convolution fusion | flops 1075314688 | bytes 5242880 | tf_op jit(solution)/shard_map/dot_general | solution.py:154
  237.7 19.5 %all-to-all-done.3 = bf16[32,32,1024]{2,1,0:T(8,128)(2,1)} async-done(((bf16[32,32,1024]{2,1,0:T(8,128)(2,1)}), bf16[32,32,1024]{2,1,0:T(8,128)(2,1)}, u32[]{:S(2)}, u32[]{:S(2)}) %all-to-all-start.3) | async-done | bytes 2097184 | tf_op jit(solution)/shard_map/all_to_all | solution.py:35
  257.2 2.0 reduce_sum.63
  259.2 13.1 %all-gather = bf16[128,1024]{1,0:T(8,128)(2,1)S(1)} all-gather(bf16[32,1024]{1,0:T(8,128)(2,1)S(1)} %reduce_sum.63), channel_id=2, replica_groups=mesh['batch'=4,'tm'=8,'space'=4] {'batch'}, dimensions={0}, use_global_device_ids=true | all-gather | bytes 327680 | tf_op jit(solution)/shard_map/all_gather | solution.py:40
  (60 shorter events, 10.1 us)
Async XLA Ops:
  0.6 112.6 %copy-start = (bf16[1024,1024]{1,0:T(8,128)(2,1)S(1)}, bf16[1024,1024]{1,0:T(8,128)(2,1)}, u32[]{:S(2)}) copy-start(bf16[1024,1024]{1,0:T(8,128)(2,1)} %param.17) | copy-start | bytes 6291460
  0.6 21.3 %all-to-all-start = ((bf16[1,16,8,4,1024]{4,3,2,0,1:T(4,128)(2,1)}), bf16[1,16,8,4,1024]{4,3,2,0,1:T(4,128)(2,1)S(1)}, u32[]{:S(2)}, u32[]{:S(2)}) async-start(bf16[1,16,8,4,1024]{4,3,2,0,1:T(4,128)(2,1)} %bitcast.156), calls=%async_computation | async-start | bytes 2097152 | tf_op jit(solution)/shard_map/all_to_all | solution.py:85
  26.9 3.9 %copy-start.8 = (f32[1024]{0:T(1024)S(1)}, f32[1024]{0:T(1024)}, u32[]{:S(2)}) copy-start(f32[1024]{0:T(1024)} %param.15) | copy-start | bytes 12292
  30.8 8.4 %copy-start.7 = (f32[2,8,32,1024]{3,2,1,0:T(8,128)S(1)}, f32[2,8,32,1024]{3,2,1,0:T(8,128)}, u32[]{:S(2)}) copy-start(f32[2,8,32,1024]{3,2,1,0:T(8,128)} %reshape.333) | copy-start | bytes 6291460
  32.9 18.5 %collective-permute-start.1 = (bf16[1,2,4,32,1024]{4,3,2,1,0:T(8,128)(2,1)S(1)}, bf16[1,2,4,32,1024]{4,3,2,1,0:T(8,128)(2,1)}, u32[]{:S(2)}, u32[]{:S(2)}) collective-permute-start(bf16[1,2,4,32,1024]{4,3,2,1,0:T(8,128)(2,1)S(1)} %get-tuple-element.134), channel_id=1, source_target_pairs={{1,0},{2,1},{3,2},{5,4},{6,5},{7,6},{9,8},{10,9},{11,10},{13,12},{... | collective-permute-start | bytes 1572872 | tf_op jit(solution)/shard_map/ppermute | solution.py:23
  34.2 20.8 %collective-permute-start = (bf16[1,2,4,32,1024]{4,3,2,1,0:T(8,128)(2,1)S(1)}, bf16[1,2,4,32,1024]{4,3,2,1,0:T(8,128)(2,1)}, u32[]{:S(2)}, u32[]{:S(2)}) collective-permute-start(bf16[1,2,4,32,1024]{4,3,2,1,0:T(8,128)(2,1)S(1)} %get-tuple-element.133), channel_id=1, source_target_pairs={{0,1},{1,2},{2,3},{4,5},{5,6},{6,7},{8,9},{9,10},{10,11},{12,13},{... | collective-permute-start | bytes 1572872 | tf_op jit(solution)/shard_map/ppermute | solution.py:22
  45.7 1.7 copy-start.3
  55.0 3.8 %slice-start = ((bf16[1,2,8,32,3072]{4,3,2,1,0:T(8,128)(2,1)}), bf16[1,2,8,32,2048]{4,3,2,1,0:T(8,128)(2,1)S(1)}, s32[]{:S(2)}) async-start(bf16[1,2,8,32,3072]{4,3,2,1,0:T(8,128)(2,1)} %copy-done.3), calls=%async_computation.4 | async-start | bytes 4194304 | tf_op jit(solution)/shard_map/slice | solution.py:100
  58.8 2.2 copy-start.11
  69.7 3.1 %copy-start.2 = (bf16[2,256,1024]{2,1,0:T(8,128)(2,1)S(1)}, bf16[2,256,1024]{2,1,0:T(8,128)(2,1)}, u32[]{:S(2)}) copy-start(bf16[2,256,1024]{2,1,0:T(8,128)(2,1)} %get-tuple-element.218) | copy-start | bytes 3145732 | tf_op jit(solution)/shard_map/while
  73.8 7.6 %copy-start.1 = (bf16[512,1024]{0,1:T(8,128)(2,1)S(1)}, bf16[512,1024]{0,1:T(8,128)(2,1)}, u32[]{:S(2)}) copy-start(bf16[512,1024]{0,1:T(8,128)(2,1)} %get-tuple-element.192) | copy-start | bytes 3145732 | tf_op jit(solution)/shard_map/while
  95.8 3.1 %copy-start.2 = (bf16[2,256,1024]{2,1,0:T(8,128)(2,1)S(1)}, bf16[2,256,1024]{2,1,0:T(8,128)(2,1)}, u32[]{:S(2)}) copy-start(bf16[2,256,1024]{2,1,0:T(8,128)(2,1)} %get-tuple-element.218) | copy-start | bytes 3145732 | tf_op jit(solution)/shard_map/while
  99.9 7.6 %copy-start.1 = (bf16[512,1024]{0,1:T(8,128)(2,1)S(1)}, bf16[512,1024]{0,1:T(8,128)(2,1)}, u32[]{:S(2)}) copy-start(bf16[512,1024]{0,1:T(8,128)(2,1)} %get-tuple-element.192) | copy-start | bytes 3145732 | tf_op jit(solution)/shard_map/while
  113.3 4.3 %copy-start.10 = (f32[1024]{0:T(1024)S(1)}, f32[1024]{0:T(1024)}, u32[]{:S(2)}) copy-start(f32[1024]{0:T(1024)} %param.18) | copy-start | bytes 12292
  116.5 1.0 copy-start.12
  129.0 4.6 %copy-start.9 = (s32[1,16]{1,0:T(1,128)S(1)}, s32[1,16]{1,0:T(1,128)}, u32[]{:S(2)}) copy-start(s32[1,16]{1,0:T(1,128)} %param.13) | copy-start | bytes 196
  129.0 49.0 %all-to-all-start.1 = ((bf16[1,2,256,3072]{3,1,0,2:T(2,128)(2,1)}), bf16[1,2,256,3072]{3,1,0,2:T(2,128)(2,1)}, u32[]{:S(2)}, u32[]{:S(2)}) async-start(bf16[1,2,256,3072]{3,1,0,2:T(2,128)(2,1)} %copy.100), calls=%async_computation.1 | async-start | bytes 6291456 | tf_op jit(solution)/shard_map/all_to_all | solution.py:143
  197.8 2.0 copy-start.6
  221.9 4.2 %copy-start.4 = (bf16[1,16,32,1024]{3,2,0,1:T(8,128)(2,1)}, bf16[1,16,32,1024]{3,2,0,1:T(8,128)(2,1)S(1)}, u32[]{:S(2)}) copy-start(bf16[1,16,32,1024]{3,2,0,1:T(8,128)(2,1)S(1)} %all_to_all.47) | copy-start | bytes 3145732
  226.2 7.3 %copy-start.5 = (bf16[1,16,32,1024]{3,2,0,1:T(8,128)(2,1)S(1)}, bf16[1,16,32,1024]{3,2,0,1:T(8,128)(2,1)}, u32[]{:S(2)}) copy-start(bf16[1,16,32,1024]{3,2,0,1:T(8,128)(2,1)} %copy-done.4) | copy-start | bytes 3145732
  226.2 31.1 %all-to-all-start.3 = ((bf16[32,32,1024]{2,1,0:T(8,128)(2,1)}), bf16[32,32,1024]{2,1,0:T(8,128)(2,1)}, u32[]{:S(2)}, u32[]{:S(2)}) async-start(bf16[32,32,1024]{2,1,0:T(8,128)(2,1)} %bitcast.154), calls=%async_computation.3 | async-start | bytes 4194304 | tf_op jit(solution)/shard_map/all_to_all | solution.py:35
where the time goes:
time: 274 us; the launch traced here: 273 us
  waiting for transfers between devices  79.1 us (29%)
  local copies, waits for them, and re-layouts  63.6 us (23%)
  matrix products  63.5 us (23%)
  blocking collectives  28.3 us (10%)
  starting transfers between devices  24.2 us (9%)
  other arithmetic  13.3 us (5%)
    all_to_all x1, waiting for transfers between devices, per_device(): lax.all_to_all(projected_two, 'tm', split_axis=2, concat_axis=1, tiled=True)  44.3 us
    all_to_all x1, waiting for transfers between devices, summed_on_arrival(): lax.all_to_all(parts, axis, split_axis=0, concat_axis=0, tiled=True)  19.5 us
    dynamic_slice x10, local copies, waits for them, and re-layouts, per_device(): lax.map(spatial_item, (projected[..., :D].reshape(item_count, tokens, D),...  17.6 us
    sub x2, matrix products, softmax_rounded(): exponent = jnp.exp(masked - top_score)  15.3 us
    all_to_all x1, waiting for transfers between devices, per_device(): lax.all_to_all(clip_tokens, 'tm', split_axis=1, concat_axis=3, tiled=True)  15.3 us
    all_to_all x1, blocking collectives, per_device(): lax.all_to_all(context_all, 'tm', split_axis=1, concat_axis=2, tiled=True)  15.3 us
    all_gather x1, blocking collectives, gathered_total(): return lax.all_gather(value, axis).astype(jnp.float32).sum(0)  13.1 us
    another operation x3, local copies, waits for them, and re-layouts  10.4 us
  transfers between devices with their start and end apart: 5, of which 3 were waited for; matrix products, arithmetic and copies ran while one was open for 7% of the time, Pallas kernels for 0%

commit v1 on v0

v1 whole, which is shorter than its diff:
```python
import functools
import math

import jax
import jax.numpy as jnp
from jax import lax
from jax.experimental import pallas as pl
from jax.experimental.pallas import tpu as pltpu
from jax.sharding import PartitionSpec as P

D = 1024
HEAD_DIM = 64
FLOOR = 0.5
TM = 8
SP = 4
FR = 2
TB = 32
HB = 16
EXT = TB + 2 * HB
PAIR = 128
NEG = -1e30
QSCALE = HEAD_DIM**-0.5 * math.log2(math.e)
MESH = pl.DeviceIdType.MESH
F32 = jnp.float32
BF16 = jnp.bfloat16


def norm_rows(values, gain):
    x = values.astype(F32)
    x = x * lax.rsqrt(jnp.mean(x * x, axis=-1, keepdims=True) + FLOOR)
    return (x * gain).astype(BF16)


def head_masks(width):
    lane = lax.broadcasted_iota(jnp.int32, (1, width), 1)
    odd = lax.rem(lane // HEAD_DIM, 2).astype(F32)
    return (1.0 - odd) * QSCALE, odd * QSCALE


def iota(shape, dim):
    return lax.broadcasted_iota(jnp.int32, shape, dim)


def softmax_times(q, k, v, bias):
    s = lax.dot_general(q, k, (((1,), (1,)), ((), ())), preferred_element_type=F32)
    s = s + bias
    top = jnp.max(s, axis=-1, keepdims=True)
    p = jnp.exp2(s - top)
    total = jnp.sum(p, axis=-1, keepdims=True)
    o = jnp.dot(p.astype(BF16), v, preferred_element_type=F32)
    return o / total


def kernel(
    order_ref,
    reach_ref,
    gain1_ref,
    gain2_ref,
    x_hbm,
    cot_hbm,
    w1_hbm,
    m1_hbm,
    w2_hbm,
    m2_hbm,
    out_hbm,
    wg_ref,
    w1,
    m1,
    w2,
    m2,
    xbuf,
    xn,
    qe,
    qo,
    kv,
    sbias,
    ctx,
    cbuf,
    xpos,
    mid,
    xn2,
    qe2,
    qo2,
    kv2,
    tbias,
    ctx2,
    cot,
    obuf,
    pbuf,
    ra,
    sa,
    rb1,
    sb1,
    rb2,
    sb2,
    rb3,
    fin,
    lsem,
    xs,
    xr,
    hs,
    hr,
    cs,
    cr,
    ts,
    tr,
    os_,
    or_,
    as_,
    ar,
    b1s,
    b1r,
    b2s,
    b2r,
    b3s,
    b3r,
):
    me = lax.axis_index("tm")
    z = lax.axis_index("space")
    batch = lax.axis_index("batch")
    core = lax.rem(batch, 2)
    mate = batch + 1 - 2 * core
    far = lax.rem(batch + 2, 4)

    def peer(d):
        return lax.rem(me + d, TM)

    def zpeer(d):
        return lax.rem(z + d, SP)

    def rcopy(src, dst, send, recv, **where):
        return pltpu.make_async_remote_copy(
            src_ref=src, dst_ref=dst, send_sem=send, recv_sem=recv, device_id=where, device_id_type=MESH
        )

    loads = [
        pltpu.make_async_copy(w1_hbm, w1, lsem.at[0]),
        pltpu.make_async_copy(x_hbm, xpos, lsem.at[1]),
        pltpu.make_async_copy(m1_hbm, m1, lsem.at[2]),
        pltpu.make_async_copy(w2_hbm, w2, lsem.at[3]),
        pltpu.make_async_copy(m2_hbm, m2, lsem.at[4]),
        pltpu.make_async_copy(cot_hbm.at[me], cot.at[:, me], lsem.at[5]),
        pltpu.make_async_copy(x_hbm.at[0, me], xbuf.at[0, me, pl.ds(HB, TB)], lsem.at[6]),
        pltpu.make_async_copy(x_hbm.at[1, me], xbuf.at[1, me, pl.ds(HB, TB)], lsem.at[7]),
    ]
    for i in (6, 7, 0, 1, 2, 3, 4, 5):
        loads[i].start()

    barrier = pltpu.get_barrier_semaphore()
    for d in range(1, TM):
        pl.semaphore_signal(barrier, inc=1, device_id={"tm": peer(d)}, device_id_type=MESH)
    for d in range(1, SP):
        pl.semaphore_signal(barrier, inc=1, device_id={"space": zpeer(d)}, device_id_type=MESH)
    pl.semaphore_signal(barrier, inc=1, device_id={"batch": mate}, device_id_type=MESH)
    pl.semaphore_signal(barrier, inc=1, device_id={"batch": far}, device_id_type=MESH)
    pl.semaphore_wait(barrier, TM - 1 + SP - 1 + 2)

    pending = []

    tok = {}
    for f in range(FR):
        for d in range(1, TM):
            t = peer(d)
            cp = rcopy(x_hbm.at[f, t], xbuf.at[f, me, pl.ds(HB, TB)], xs.at[f, d], xr.at[f, d], tm=t)
            cp.start()
            tok[f, d] = cp
            pending.append(cp)
    cots = []
    for d in range(1, TM):
        t = peer(d)
        cp = rcopy(cot_hbm.at[t], cot.at[:, me], cs.at[d], cr.at[d], tm=t)
        cp.start()
        cots.append(cp)
        pending.append(cp)

    order_col = jnp.zeros((256, 1), jnp.int32)
    order_row = jnp.zeros((1, 256), jnp.int32)
    col_slot = iota((256, 1), 0) // 16
    row_slot = iota((1, 256), 1) // 16
    for f in range(FR):
        for s in range(TM):
            value = order_ref[0, s * FR + f]
            order_col = jnp.where(col_slot == f * TM + s, value, order_col)
            order_row = jnp.where(row_slot == f * TM + s, value, order_row)
    same = lax.rem(iota((256, 256), 0), 16) == lax.rem(iota((256, 256), 1), 16)
    tbias[...] = jnp.where(same & (order_row <= order_col), 0.0, NEG)
    key = iota((128, 384), 1)
    key_src = jnp.zeros((128, 384), jnp.int32)
    for n in range(1, TM):
        key_src = key_src + (key >= 48 * n).astype(jnp.int32)
    key_row = (key - 48 * key_src) // 4 - 4
    query_row = lax.rem(iota((128, 384), 0), 16) // 4
    distance = jnp.abs(key_row - query_row)
    for f in range(FR):
        for h in range(2):
            row = key_row + (z * 8 + 4 * h)
            keep = (distance <= reach_ref[0, f]) & (row >= 0) & (row < 8 * SP)
            sbias[f, h] = jnp.where(keep, 0.0, NEG)

    even_mask, odd_mask = head_masks(256)

    halo = {}

    def forward(f):
        for d in range(TM):
            if d == 0:
                loads[6 + f].wait()
            else:
                tok[f, d].wait_recv()
            s = lax.rem(me + TM - d, TM)
            up = rcopy(
                xbuf.at[f, s, pl.ds(HB, HB)],
                xbuf.at[f, s, pl.ds(HB + TB, HB)],
                hs.at[f, d, 0],
                hr.at[f, d, 0],
                space=zpeer(SP - 1),
            )
            down = rcopy(
                xbuf.at[f, s, pl.ds(TB, HB)],
                xbuf.at[f, s, pl.ds(0, HB)],
                hs.at[f, d, 1],
                hr.at[f, d, 1],
                space=zpeer(1),
            )
            up.start()
            down.start()
            halo[f, d] = (up, down)
            pending.extend((up, down))

    def project_own(f):
        xn[...] = norm_rows(xbuf[f, :, HB : HB + TB].reshape(TM * TB, D), gain1_ref[...])

        @pl.loop(0, 4)
        def _(n):
            at = pl.ds(pl.multiple_of(n * 256, 256), 256)
            acc = jnp.dot(xn[...], w1[:, at], preferred_element_type=F32)
            qe[:, :, at] = (acc * even_mask).astype(BF16).reshape(TM, TB, 256)
            qo[:, :, at] = (acc * odd_mask).astype(BF16).reshape(TM, TB, 256)

        @pl.loop(0, 8)
        def _(n):
            at = pl.ds(pl.multiple_of(n * 256, 256), 256)
            wat = pl.ds(pl.multiple_of(n * 256 + D, 256), 256)
            acc = jnp.dot(xn[...], w1[:, wat], preferred_element_type=F32)
            kv[:, HB : HB + TB, at] = acc.astype(BF16).reshape(TM, TB, 256)

    def project_halo(f):
        for d in range(TM):
            halo[f, d][0].wait_recv()
            halo[f, d][1].wait_recv()
        half = TM * HB
        xn[:half] = norm_rows(xbuf[f, :, :HB].reshape(half, D), gain1_ref[...])
        xn[half:] = norm_rows(xbuf[f, :, HB + TB :].reshape(half, D), gain1_ref[...])

        @pl.loop(0, 8)
        def _(n):
            at = pl.ds(pl.multiple_of(n * 256, 256), 256)
            wat = pl.ds(pl.multiple_of(n * 256 + D, 256), 256)
            acc = jnp.dot(xn[...], w1[:, wat], preferred_element_type=F32).astype(BF16)
            kv[:, :HB, at] = acc[:half].reshape(TM, HB, 256)
            kv[:, HB + TB :, at] = acc[half:].reshape(TM, HB, 256)

    lane_even = iota((1, PAIR), 1) < HEAD_DIM

    def attend(f):
        @pl.loop(0, 8)
        def _(n):
            at = pl.ds(pl.multiple_of(n * PAIR, PAIR), PAIR)
            vat = pl.ds(pl.multiple_of(n * PAIR + D, PAIR), PAIR)
            for h in range(2):
                rows = slice(h * HB, (h + 1) * HB)
                keys = slice(h * HB, h * HB + 3 * HB)
                k = kv[:, keys, at].reshape(384, PAIR)
                v = kv[:, keys, vat].reshape(384, PAIR)
                o = []
                for q in (qe, qo):
                    o.append(softmax_times(q[:, rows, at].reshape(128, PAIR), k, v, sbias[f, h]))
                both = jnp.where(lane_even, o[0], o[1]).astype(BF16)
                ctx[f, :, rows, at] = both.reshape(TM, HB, PAIR)

    back = {}

    def send_context(f):
        for d in range(1, TM):
            t = peer(d)
            cp = rcopy(ctx.at[f, t], cbuf.at[f, me], ts.at[f, d], tr.at[f, d], tm=t)
            cp.start()
            back[f, d] = cp
            pending.append(cp)

    forward(0)
    loads[0].wait()
    project_own(0)
    forward(1)
    project_halo(0)
    attend(0)
    send_context(0)
    project_own(1)
    project_halo(1)
    attend(1)
    send_context(1)

    loads[1].wait()
    loads[2].wait()
    loads[3].wait()

    for f in range(FR):
        cbuf[f, me] = ctx[f, me]
        for d in range(1, TM):
            back[f, d].wait_recv()

        @pl.loop(0, 4)
        def _(n):
            at = pl.ds(pl.multiple_of(n * 256, 256), 256)
            acc = jnp.dot(cbuf[f].reshape(TM * TB, D), m1[:, at], preferred_element_type=F32)
            acc = acc + xpos[f, :, :, at].reshape(TM * TB, 256).astype(F32)
            mid[f, :, at] = acc.astype(BF16)

        xn2[...] = norm_rows(mid[f], gain2_ref[...])

        @pl.loop(0, 4)
        def _(n):
            at = pl.ds(pl.multiple_of(n * 256, 256), 256)
            acc = jnp.dot(xn2[...], w2[:, at], preferred_element_type=F32)
            qe2[f, :, :, at] = (acc * even_mask).astype(BF16).reshape(TM, TB, 256)
            qo2[f, :, :, at] = (acc * odd_mask).astype(BF16).reshape(TM, TB, 256)

        @pl.loop(0, 8)
        def _(n):
            at = pl.ds(pl.multiple_of(n * 256, 256), 256)
            wat = pl.ds(pl.multiple_of(n * 256 + D, 256), 256)
            acc = jnp.dot(xn2[...], w2[:, wat], preferred_element_type=F32)
            kv2[f, :, :, at] = acc.astype(BF16).reshape(TM, TB, 256)

    loads[5].wait()
    for cp in cots:
        cp.wait_recv()

    first = []
    for g in range(4):

        @pl.loop(0, 2)
        def _(i):
            n = g * 2 + i
            at = pl.ds(pl.multiple_of(n * PAIR, PAIR), PAIR)
            vat = pl.ds(pl.multiple_of(n * PAIR + D, PAIR), PAIR)
            for b in range(2):
                rows = slice(b * 16, (b + 1) * 16)
                k = kv2[:, :, rows, at].reshape(256, PAIR)
                v = kv2[:, :, rows, vat].reshape(256, PAIR)
                o = []
                for q in (qe2, qo2):
                    o.append(softmax_times(q[:, :, rows, at].reshape(256, PAIR), k, v, tbias[...]))
                both = jnp.where(lane_even, o[0], o[1]).astype(BF16)
                ctx2[:, :, rows, at] = both.reshape(FR, TM, 16, PAIR)

        a = ctx2[:, :, :, g * 256 : (g + 1) * 256].reshape(FR * TM * TB, 256)

        @pl.loop(0, 4)
        def _(n):
            at = pl.ds(pl.multiple_of(n * 256, 256), 256)
            c = cot[:, :, :, at].reshape(FR * TM * TB, 256)
            acc = lax.dot_general(a, c, (((0,), (0,)), ((), ())), preferred_element_type=F32)
            pbuf[g * 2 : g * 2 + 2, :, :, :, at] = acc.astype(BF16).reshape(2, SP, 2, 16, 256)

        cp = rcopy(
            pbuf.at[pl.ds(g * 2, 2), :, 1 - core], ra.at[pl.ds(g * 2, 2)], as_.at[g], ar.at[g], batch=mate
        )
        cp.start()
        pending.append(cp)
        first.append(cp)
        if g > 0:
            reduce_rows(g - 1, first, pbuf, ra, sa, core)
            start_z(g - 1, sa, rb1, b1s, b1r, rcopy, zpeer, pending)
    loads[4].wait()
    outs = []
    for f in range(FR):

        @pl.loop(0, 4)
        def _(n):
            at = pl.ds(pl.multiple_of(n * 256, 256), 256)
            acc = jnp.dot(ctx2[f].reshape(TM * TB, D), m2[:, at], preferred_element_type=F32)
            acc = acc + mid[f, :, at].astype(F32)
            obuf[f, :, :, at] = acc.astype(BF16).reshape(TM, TB, 256)

        own = pltpu.make_async_copy(obuf.at[f, me], out_hbm.at[f, me], lsem.at[8 + f])
        own.start()
        outs.append(own)
        for d in range(1, TM):
            t = peer(d)
            cp = rcopy(obuf.at[f, t], out_hbm.at[f, me], os_.at[f, d], or_.at[f, d], tm=t)
            cp.start()
            outs.append(cp)
        if f == 0:
            reduce_rows(3, first, pbuf, ra, sa, core)
            start_z(3, sa, rb1, b1s, b1r, rcopy, zpeer, pending)

    last = []
    for g in range(4):
        for d in range(1, SP):
            rcopy(
                sa.at[pl.ds(g * 2, 2), zpeer(d)],
                rb1.at[d - 1, pl.ds(g * 2, 2)],
                b1s.at[g, d - 1],
                b1r.at[g, d - 1],
                space=zpeer(d),
            ).wait_recv()
        total = sa[pl.ds(g * 2, 2), z].astype(F32)
        for d in range(1, SP):
            total = total + rb1[d - 1, pl.ds(g * 2, 2)].astype(F32)
        sb1[pl.ds(g * 2, 2)] = total.astype(BF16)
    for d in range(1, TM):
        t = peer(d)
        cp = rcopy(sb1.at[t], rb2.at[d - 1], b2s.at[d], b2r.at[d], tm=t)
        cp.start()
        last.append(cp)
        pending.append(cp)
    total = sb1[me].astype(F32)
    for d in range(1, TM):
        last[d - 1].wait_recv()
        total = total + rb2[d - 1].astype(F32)
    sb2[...] = total.astype(BF16)
    cp = rcopy(sb2, rb3, b3s.at[0], b3r.at[0], batch=far)
    cp.start()
    cp.wait()
    fin[core] = sb2[...].astype(F32) + rb3[...].astype(F32)
    cp = rcopy(fin.at[core], fin.at[core], b3s.at[1], b3r.at[1], batch=mate)
    cp.start()
    cp.wait()
    wg_ref[...] = fin[...].reshape(32, D)

    for cp in pending:
        cp.wait_send()
    for cp in outs:
        cp.wait()


def reduce_rows(g, first, pbuf, ra, sa, core):
    first[g].wait_recv()
    rows = pl.ds(g * 2, 2)
    sa[rows] = (pbuf[rows, :, core].astype(F32) + ra[rows].astype(F32)).astype(BF16)


def start_z(g, sa, rb1, b1s, b1r, rcopy, zpeer, pending):
    rows = pl.ds(g * 2, 2)
    for d in range(1, SP):
        cp = rcopy(
            sa.at[rows, zpeer(d)], rb1.at[d - 1, rows], b1s.at[g, d - 1], b1r.at[g, d - 1], space=zpeer(d)
        )
        cp.start()
        pending.append(cp)


def per_device(
    clip_tokens,
    frame_order,
    row_reach,
    spatial_gain,
    spatial_heads,
    spatial_merge,
    temporal_gain,
    temporal_heads,
    temporal_merge,
    cotangent,
):
    tokens = clip_tokens.reshape(TM, FR, TB, D).transpose(1, 0, 2, 3)
    grads = cotangent.reshape(FR, 8, TM, 4, D).transpose(2, 0, 1, 3, 4).reshape(TM, FR, TB, D)
    dma = pltpu.SemaphoreType.DMA
    vm = pltpu.VMEM
    smem = pl.BlockSpec(memory_space=pltpu.SMEM)
    vmem = pl.BlockSpec(memory_space=pltpu.VMEM)
    anym = pl.BlockSpec(memory_space=pl.ANY)
    out, wg = pl.pallas_call(
        kernel,
        out_shape=[
            jax.ShapeDtypeStruct((FR, TM, TB, D), BF16),
            jax.ShapeDtypeStruct((32, D), F32),
        ],
        in_specs=[smem, smem, vmem, vmem] + [anym] * 6,
        out_specs=[anym, vmem],
        scratch_shapes=[
            vm((D, 3 * D), BF16),
            vm((D, D), BF16),
            vm((D, 3 * D), BF16),
            vm((D, D), BF16),
            vm((FR, TM, EXT, D), BF16),
            vm((TM * TB, D), BF16),
            vm((TM, TB, D), BF16),
            vm((TM, TB, D), BF16),
            vm((TM, EXT, 2 * D), BF16),
            vm((FR, 2, 128, 384), F32),
            vm((FR, TM, TB, D), BF16),
            vm((FR, TM, TB, D), BF16),
            vm((FR, TM, TB, D), BF16),
            vm((FR, TM * TB, D), BF16),
            vm((TM * TB, D), BF16),
            vm((FR, TM, TB, D), BF16),
            vm((FR, TM, TB, D), BF16),
            vm((FR, TM, TB, 2 * D), BF16),
            vm((256, 256), F32),
            vm((FR, TM, TB, D), BF16),
            vm((FR, TM, TB, D), BF16),
            vm((FR, TM, TB, D), BF16),
            vm((TM, SP, 2, 16, D), BF16),
            vm((TM, SP, 16, D), BF16),
            vm((TM, SP, 16, D), BF16),
            vm((SP - 1, TM, 16, D), BF16),
            vm((TM, 16, D), BF16),
            vm((TM - 1, 16, D), BF16),
            vm((16, D), BF16),
            vm((16, D), BF16),
            vm((2, 16, D), F32),
            dma((10,)),
            dma((FR, TM)),
            dma((FR, TM)),
            dma((FR, TM, 2)),
            dma((FR, TM, 2)),
            dma((TM,)),
            dma((TM,)),
            dma((FR, TM)),
            dma((FR, TM)),
            dma((FR, TM)),
            dma((FR, TM)),
            dma((4,)),
            dma((4,)),
            dma((4, SP - 1)),
            dma((4, SP - 1)),
            dma((TM,)),
            dma((TM,)),
            dma((2,)),
            dma((2,)),
        ],
        compiler_params=pltpu.CompilerParams(
            collective_id=0, has_side_effects=True, vmem_limit_bytes=62 * 1024 * 1024
        ),
    )(
        frame_order,
        row_reach,
        spatial_gain.reshape(1, D),
        temporal_gain.reshape(1, D),
        tokens,
        grads,
        spatial_heads,
        spatial_merge,
        temporal_heads,
        temporal_merge,
    )
    out = out.reshape(FR, TM, 8, 4, D).transpose(0, 2, 1, 3, 4).reshape(1, FR, 8, 32, D)
    return out, wg


def solution(mesh):
    in_specs = (
        P("batch", None, "space", "tm", None),
        P("batch", None),
        P("batch", "tm"),
        P(),
        P(),
        P(),
        P(),
        P(),
        P(),
        P("batch", "tm", "space", None, None),
    )
    out_specs = (P("batch", "tm", "space", None, None), P(("tm", "space"), None))
    return jax.shard_map(
        per_device, mesh=mesh, in_specs=in_specs, out_specs=out_specs, check_vma=False
    )
```

time: 274 us -> 118 us (0.43)
  Pallas kernels: 0 us -> 108 us
  waiting for transfers between devices: 79.1 us -> 0 us
  matrix products: 63.5 us -> 0 us
  local copies, waits for them, and re-layouts: 63.6 us -> 9.2 us
  blocking collectives: 28.3 us -> 0 us
  starting transfers between devices: 24.2 us -> 0 us
  other arithmetic: 13.3 us -> 0 us
    pallas_call x0 -> x1, Pallas kernels: none -> 108 us  [per_device(): pl.pallas_call(kernel, out_shape=[jax.ShapeDtypeStruct((FR, TM, TB, D), B...]
    all_to_all x3 -> x0, waiting for transfers between devices: 79.1 us -> none  [the longest x1 44.3 us: per_device(): lax.all_to_all(projected_two, 'tm', split_axis=2, concat_axis=1, tiled=True)]
    dot_general x11 -> x0, matrix products: 48.2 us -> none  [the longest x2 9.73 us: spatial_item(): jnp.einsum('hqk,khd->qhd', weights, value_heads, preferred_element_type=j...]
    convert_element_type x6 -> x0, local copies, waits for them, and re-layouts: 19 us -> none  [the longest x2 5.97 us: normalize(): widened = values.astype(jnp.float32)]
    all_to_all x3 -> x0, starting transfers between devices: 17.9 us -> none  [the longest x1 7.33 us: summed_on_arrival(): lax.all_to_all(parts, axis, split_axis=0, concat_axis=0, tiled=True)]
    dynamic_slice x10 -> x0, local copies, waits for them, and re-layouts: 17.6 us -> none  [per_device(): lax.map(spatial_item, (projected[..., :D].reshape(item_count, tokens, D),...]
    sub x2 -> x0, matrix products: 15.3 us -> none  [softmax_rounded(): exponent = jnp.exp(masked - top_score)]
    all_to_all x1 -> x0, blocking collectives: 15.3 us -> none  [per_device(): lax.all_to_all(context_all, 'tm', split_axis=1, concat_axis=2, tiled=True)]
  transfers between devices with their start and end apart: 5 -> 0, of which waited for: 3 -> 0; matrix products, arithmetic and copies ran while one was open for 7% -> 0% of each run, Pallas kernels for 0% -> 0%
where the time goes in v1:
time: 118 us; the launch traced here: 117 us
  Pallas kernels  108 us (92%)
  local copies, waits for them, and re-layouts  9.2 us (8%)
    pallas_call x1, Pallas kernels, per_device(): pl.pallas_call(kernel, out_shape=[jax.ShapeDtypeStruct((FR, TM, TB, D), B...  108 us
    reshape x3, local copies, waits for them, and re-layouts, per_device(): cotangent.reshape(FR, 8, TM, 4, D).transpose(2, 0, 1, 3, 4)  3.05 us
    reshape x2, local copies, waits for them, and re-layouts, per_device(): out.reshape(FR, TM, 8, 4, D).transpose(0, 2, 1, 3, 4)  2.6 us
    reshape x2, local copies, waits for them, and re-layouts, per_device(): tokens = clip_tokens.reshape(TM, FR, TB, D).transpose(1, 0, 2, 3)  2.41 us

profile of v1, /device:TPU:1, one launch (start us, length us, event | category | flops | bytes accessed | tf_op | source)
XLA Modules:
  0.0 117.4 jit_solution(8901447000851493662)
XLA Ops:
  0.6 1.3 %reshape.27 = bf16[8,2,32,1024]{3,2,1,0:T(8,128)(2,1)S(1)} reshape(bf16[1,16,8,4,1024]{4,3,2,1,0:T(4,128)(2,1)} %param.10) | data formatting | bytes 2097152 | tf_op jit(solution)/shard_map/reshape | solution.py:466
  2.0 1.1 copy.20
  3.0 1.5 %reshape.28 = bf16[2,8,8,4,1024]{4,3,2,1,0:T(4,128)(2,1)S(1)} reshape(bf16[1,2,8,32,1024]{4,3,2,1,0:T(8,128)(2,1)} %param.19) | data formatting | bytes 2097152 | tf_op jit(solution)/shard_map/reshape | solution.py:467
  4.5 0.5 copy.19
  5.0 1.1 reshape.29.cot_hbm
  6.1 107.5 %shard_map.113 = (bf16[2,8,32,1024]{3,2,1,0:T(8,128)(2,1)}, f32[32,1024]{1,0:T(8,128)}) custom-call(s32[1,16]{1,0:T(1,128)} %order_ref.1, s32[1,2]{1,0:T(1,128)} %reach_ref.1, f32[1,1024]{1,0:T(1,128)} %bitcast.16, f32[1,1024]{1,0:T(1,128)} %bitcast.17, bf16[2,8,32,1024]{3,2,1,0:T(8,128)(2,1)} %bitcast.13, bf16[8,2,32,1024]{3,2,1,0:T(8,128)(2,1)} %reshape.29.cot_hbm, ...), custom_call_target="tpu_custom_call" | custom-call | tf_op jit(solution)/shard_map/pallas_call | solution.py:473
  113.6 0.0 copy-start
  113.6 1.5 %reshape.30 = bf16[2,8,8,4,1024]{4,3,2,1,0:T(4,128)(2,1)S(1)} reshape(bf16[2,8,32,1024]{3,2,1,0:T(8,128)(2,1)} %get-tuple-element.4) | data formatting | bytes 2097152 | tf_op jit(solution)/shard_map/reshape | solution.py:548
  115.1 0.5 copy.16
  115.6 1.1 reshape.31
  116.7 0.0 copy-done
  116.7 0.7 copy.22
Async XLA Ops:
  113.6 3.1 %copy-start = (f32[32,1024]{1,0:T(8,128)S(1)}, f32[32,1024]{1,0:T(8,128)}, u32[]{:S(2)}) copy-start(f32[32,1024]{1,0:T(8,128)} %get-tuple-element.9) | copy-start | bytes 393220

commit v2 on v1

v2 whole, which is shorter than its diff:
```python
import functools
import math

import jax
import jax.numpy as jnp
from jax import lax
from jax.experimental import pallas as pl
from jax.experimental.pallas import tpu as pltpu
from jax.sharding import PartitionSpec as P

D = 1024
HEAD_DIM = 64
FLOOR = 0.5
TM = 8
SP = 4
FR = 2
TB = 32
HB = 16
EXT = TB + 2 * HB
PAIR = 128
WIDE = 1024
GROUP = 2
NEG = -1e30
QSCALE = HEAD_DIM**-0.5 * math.log2(math.e)
MESH = pl.DeviceIdType.MESH
F32 = jnp.float32
BF16 = jnp.bfloat16


def unrolled(count):
    def run(body):
        for n in range(count):
            body(n)

    return run


def norm_rows(values, gain):
    x = values.astype(F32)
    x = x * lax.rsqrt(jnp.mean(x * x, axis=-1, keepdims=True) + FLOOR)
    return (x * gain).astype(BF16)


def head_masks(width):
    lane = lax.broadcasted_iota(jnp.int32, (1, width), 1)
    odd = lax.rem(lane // HEAD_DIM, 2).astype(F32)
    return (1.0 - odd) * QSCALE, odd * QSCALE


def iota(shape, dim):
    return lax.broadcasted_iota(jnp.int32, shape, dim)


def attend(chains):
    scores = [
        lax.dot_general(k, q, (((1,), (1,)), ((), ())), preferred_element_type=F32) + bias
        for q, k, _, bias in chains
    ]
    weights = []
    for s in scores:
        p = jnp.exp2(s - jnp.max(s, axis=0, keepdims=True))
        weights.append((p.astype(BF16), 1.0 / jnp.sum(p, axis=0, keepdims=True)))
    outputs = []
    for (q, _, v, _), (p, scale) in zip(chains, weights):
        count = q.shape[0] // 2
        o = lax.dot_general(v, p, (((0,), (0,)), ((), ())), preferred_element_type=F32) * scale
        both = jnp.where(iota((PAIR, count), 0) < HEAD_DIM, o[:, :count], o[:, count:])
        outputs.append(both.T.astype(BF16))
    return outputs


def kernel(
    order_ref,
    reach_ref,
    gain1_ref,
    gain2_ref,
    x_hbm,
    cot_hbm,
    w1_hbm,
    m1_hbm,
    w2_hbm,
    m2_hbm,
    out_hbm,
    wg_ref,
    w1,
    m1,
    w2,
    m2,
    xbuf,
    xn,
    qe,
    qo,
    kv,
    sbias,
    ctx,
    cbuf,
    xpos,
    mid,
    xn2,
    qe2,
    qo2,
    kv2,
    tbias,
    ctx2,
    cot,
    obuf,
    pbuf,
    ra,
    sa,
    rb1,
    sb1,
    rb2,
    sb2,
    rb3,
    lsem,
    xs,
    xr,
    hs,
    hr,
    cs,
    cr,
    ts,
    tr,
    os_,
    or_,
    as_,
    ar,
    b1s,
    b1r,
    b2s,
    b2r,
    b3s,
    b3r,
):
    me = lax.axis_index("tm")
    z = lax.axis_index("space")
    batch = lax.axis_index("batch")
    core = lax.rem(batch, 2)
    mate = batch + 1 - 2 * core
    others = (lax.rem(batch + 2, 4), mate, lax.rem(mate + 2, 4))

    def peer(d):
        return lax.rem(me + d, TM)

    def zpeer(d):
        return lax.rem(z + d, SP)

    def rcopy(src, dst, send, recv, **where):
        return pltpu.make_async_remote_copy(
            src_ref=src, dst_ref=dst, send_sem=send, recv_sem=recv, device_id=where, device_id_type=MESH
        )

    loads = [
        pltpu.make_async_copy(w1_hbm, w1, lsem.at[0]),
        pltpu.make_async_copy(x_hbm, xpos, lsem.at[1]),
        pltpu.make_async_copy(m1_hbm, m1, lsem.at[2]),
        pltpu.make_async_copy(w2_hbm, w2, lsem.at[3]),
        pltpu.make_async_copy(m2_hbm, m2, lsem.at[4]),
        pltpu.make_async_copy(cot_hbm.at[me], cot.at[:, me], lsem.at[5]),
        pltpu.make_async_copy(x_hbm.at[0, me], xbuf.at[0, me, pl.ds(HB, TB)], lsem.at[6]),
        pltpu.make_async_copy(x_hbm.at[1, me], xbuf.at[1, me, pl.ds(HB, TB)], lsem.at[7]),
    ]
    for i in (6, 7, 0, 1, 2, 3, 4, 5):
        loads[i].start()

    barrier = pltpu.get_barrier_semaphore()
    for d in range(1, TM):
        pl.semaphore_signal(barrier, inc=1, device_id={"tm": peer(d)}, device_id_type=MESH)
    for d in range(1, SP):
        pl.semaphore_signal(barrier, inc=1, device_id={"space": zpeer(d)}, device_id_type=MESH)
    for other in others:
        pl.semaphore_signal(barrier, inc=1, device_id={"batch": other}, device_id_type=MESH)
    with jax.named_scope("barrier"):
        pl.semaphore_wait(barrier, TM - 1 + SP - 1 + 3)

    pending = []

    tok = {}
    for f in range(FR):
        for d in range(1, TM):
            t = peer(d)
            cp = rcopy(x_hbm.at[f, t], xbuf.at[f, me, pl.ds(HB, TB)], xs.at[f, d], xr.at[f, d], tm=t)
            cp.start()
            tok[f, d] = cp
            pending.append(cp)
    cots = []

    def send_cotangent(f):
        for d in range(1, TM):
            t = peer(d)
            cp = rcopy(cot_hbm.at[t, f], cot.at[f, me], cs.at[f, d], cr.at[f, d], tm=t)
            cp.start()
            cots.append(cp)
            pending.append(cp)

    send_cotangent(0)

    order_key = jnp.zeros((256, 1), jnp.int32)
    order_query = jnp.zeros((1, 512), jnp.int32)
    key_slot = iota((256, 1), 0) // 16
    query_slot = lax.rem(iota((1, 512), 1) // 16, 16)
    for f in range(FR):
        for s in range(TM):
            value = order_ref[0, s * FR + f]
            order_key = jnp.where(key_slot == f * TM + s, value, order_key)
            order_query = jnp.where(query_slot == f * TM + s, value, order_query)
    same = lax.rem(iota((256, 512), 0), 16) == lax.rem(iota((256, 512), 1), 16)
    tbias[...] = jnp.where(same & (order_key <= order_query), 0.0, NEG)
    key = iota((384, 1), 0)
    key_src = jnp.zeros((384, 1), jnp.int32)
    for n in range(1, TM):
        key_src = key_src + (key >= 48 * n).astype(jnp.int32)
    key_row = (key - 48 * key_src) // 4 - 4
    query_row = lax.rem(iota((1, 256), 1), 16) // 4
    distance = jnp.abs(key_row - query_row)
    for f in range(FR):
        for h in range(2):
            row = key_row + (z * 8 + 4 * h)
            keep = (distance <= reach_ref[0, f]) & (row >= 0) & (row < 8 * SP)
            sbias[f, h] = jnp.where(keep, 0.0, NEG)

    even_mask, odd_mask = head_masks(WIDE)

    halo = {}

    def forward(f):
        for d in range(TM):
            if d == 0:
                loads[6 + f].wait()
            else:
                tok[f, d].wait_recv()
            s = lax.rem(me + TM - d, TM)
            up = rcopy(
                xbuf.at[f, s, pl.ds(HB, HB)],
                xbuf.at[f, s, pl.ds(HB + TB, HB)],
                hs.at[f, d, 0],
                hr.at[f, d, 0],
                space=zpeer(SP - 1),
            )
            down = rcopy(
                xbuf.at[f, s, pl.ds(TB, HB)],
                xbuf.at[f, s, pl.ds(0, HB)],
                hs.at[f, d, 1],
                hr.at[f, d, 1],
                space=zpeer(1),
            )
            up.start()
            down.start()
            halo[f, d] = (up, down)
            pending.extend((up, down))

    def project_own(f):
        xn[...] = norm_rows(xbuf[f, :, HB : HB + TB].reshape(TM * TB, D), gain1_ref[...])

        @unrolled(D // WIDE)
        def _(n):
            at = slice(n * WIDE, (n + 1) * WIDE)
            acc = jnp.dot(xn[...], w1[:, at], preferred_element_type=F32)
            qe[:, :, at] = (acc * even_mask).astype(BF16).reshape(TM, TB, WIDE)
            qo[:, :, at] = (acc * odd_mask).astype(BF16).reshape(TM, TB, WIDE)

        @unrolled(2 * D // WIDE)
        def _(n):
            at = slice(n * WIDE, (n + 1) * WIDE)
            wat = slice(n * WIDE + D, (n + 1) * WIDE + D)
            acc = jnp.dot(xn[...], w1[:, wat], preferred_element_type=F32)
            kv[:, HB : HB + TB, at] = acc.astype(BF16).reshape(TM, TB, WIDE)

    def project_halo(f):
        for d in range(TM):
            halo[f, d][0].wait_recv()
            halo[f, d][1].wait_recv()
        half = TM * HB
        xn[:half] = norm_rows(xbuf[f, :, :HB].reshape(half, D), gain1_ref[...])
        xn[half:] = norm_rows(xbuf[f, :, HB + TB :].reshape(half, D), gain1_ref[...])

        @unrolled(2 * D // WIDE)
        def _(n):
            at = slice(n * WIDE, (n + 1) * WIDE)
            wat = slice(n * WIDE + D, (n + 1) * WIDE + D)
            acc = jnp.dot(xn[...], w1[:, wat], preferred_element_type=F32).astype(BF16)
            kv[:, :HB, at] = acc[:half].reshape(TM, HB, WIDE)
            kv[:, HB + TB :, at] = acc[half:].reshape(TM, HB, WIDE)

    def attend_space(f, part):
        @pl.loop(part * 4 // GROUP, (part + 1) * 4 // GROUP)
        def _(m):
            places, chains = [], []
            for u in range(GROUP):
                at = pl.ds(pl.multiple_of((m * GROUP + u) * PAIR, PAIR), PAIR)
                vat = pl.ds(pl.multiple_of((m * GROUP + u) * PAIR + D, PAIR), PAIR)
                for h in range(2):
                    rows = slice(h * HB, (h + 1) * HB)
                    keys = slice(h * HB, h * HB + 3 * HB)
                    q = [ref[:, rows, at].reshape(128, PAIR) for ref in (qe, qo)]
                    k = kv[:, keys, at].reshape(384, PAIR)
                    v = kv[:, keys, vat].reshape(384, PAIR)
                    places.append((rows, at))
                    chains.append((jnp.concatenate(q, axis=0), k, v, sbias[f, h]))
            for (rows, at), both in zip(places, attend(chains)):
                ctx[f, :, rows, at] = both.reshape(TM, HB, PAIR)

    back = {}

    def send_context(f):
        for d in range(1, TM):
            t = peer(d)
            cp = rcopy(ctx.at[f, t], cbuf.at[f, me], ts.at[f, d], tr.at[f, d], tm=t)
            cp.start()
            back[f, d] = cp
            pending.append(cp)

    scope = jax.named_scope
    with scope("forward0"):
        forward(0)
    with scope("w1_wait"):
        loads[0].wait()
    with scope("own0"):
        project_own(0)
    with scope("halo0"):
        project_halo(0)
    with scope("attend0"):
        attend_space(0, 0)
    with scope("forward1"):
        forward(1)
    with scope("attend0"):
        attend_space(0, 1)
    with scope("send0"):
        send_context(0)
    with scope("own1"):
        project_own(1)
    with scope("halo1"):
        project_halo(1)
    with scope("attend1"):
        attend_space(1, 0)
        attend_space(1, 1)
    with scope("send1"):
        send_context(1)
        send_cotangent(1)

    loads[1].wait()
    loads[2].wait()
    loads[3].wait()

    def merge(f):
        with scope("wait_ctx"):
            cbuf[f, me] = ctx[f, me]
            for d in range(1, TM):
                back[f, d].wait_recv()

        with scope("merge"):

            @unrolled(D // WIDE)
            def _(n):
                at = slice(n * WIDE, (n + 1) * WIDE)
                acc = jnp.dot(cbuf[f].reshape(TM * TB, D), m1[:, at], preferred_element_type=F32)
                acc = acc + xpos[f, :, :, at].reshape(TM * TB, WIDE).astype(F32)
                mid[f, :, at] = acc.astype(BF16)

            xn2[...] = norm_rows(mid[f], gain2_ref[...])

        with scope("qkv2"):

            @unrolled(D // WIDE)
            def _(n):
                at = slice(n * WIDE, (n + 1) * WIDE)
                acc = jnp.dot(xn2[...], w2[:, at], preferred_element_type=F32)
                qe2[f, :, :, at] = (acc * even_mask).astype(BF16).reshape(TM, TB, WIDE)
                qo2[f, :, :, at] = (acc * odd_mask).astype(BF16).reshape(TM, TB, WIDE)

            @unrolled(2 * D // WIDE)
            def _(n):
                at = slice(n * WIDE, (n + 1) * WIDE)
                wat = slice(n * WIDE + D, (n + 1) * WIDE + D)
                acc = jnp.dot(xn2[...], w2[:, wat], preferred_element_type=F32)
                kv2[f, :, :, at] = acc.astype(BF16).reshape(TM, TB, WIDE)

    def temporal(g):
        places, chains = [], []
        for n in (2 * g, 2 * g + 1):
            at = slice(n * PAIR, (n + 1) * PAIR)
            vat = slice(n * PAIR + D, (n + 1) * PAIR + D)
            for b in range(2):
                rows = slice(b * 16, (b + 1) * 16)
                q = [ref[:, :, rows, at].reshape(256, PAIR) for ref in (qe2, qo2)]
                k = kv2[:, :, rows, at].reshape(256, PAIR)
                v = kv2[:, :, rows, vat].reshape(256, PAIR)
                places.append((rows, at))
                chains.append((jnp.concatenate(q, axis=0), k, v, tbias[...]))
        for (rows, at), both in zip(places, attend(chains)):
            ctx2[:, :, rows, at] = both.reshape(FR, TM, 16, PAIR)

    first = []

    def gradient(g):
        a = ctx2[:, :, :, g * 256 : (g + 1) * 256].reshape(FR * TM * TB, 256)

        @unrolled(D // WIDE)
        def _(n):
            at = slice(n * WIDE, (n + 1) * WIDE)
            c = cot[:, :, :, at].reshape(FR * TM * TB, WIDE)
            acc = lax.dot_general(a, c, (((0,), (0,)), ((), ())), preferred_element_type=F32)
            pbuf[g * 2 : g * 2 + 2, :, :, :, at] = acc.astype(BF16).reshape(2, SP, 2, 16, WIDE)

        cp = rcopy(
            pbuf.at[pl.ds(g * 2, 2), :, 1 - core], ra.at[pl.ds(g * 2, 2)], as_.at[g], ar.at[g], batch=mate
        )
        cp.start()
        pending.append(cp)
        first.append(cp)

    over_z = {}

    def reduce_core(g):
        with scope("reduce_core"):
            first[g].wait_recv()
            rows = pl.ds(g * 2, 2)
            sa[rows] = (pbuf[rows, :, core].astype(F32) + ra[rows].astype(F32)).astype(BF16)
            for d in range(1, SP):
                cp = rcopy(
                    sa.at[rows, zpeer(d)], rb1.at[d - 1, rows], b1s.at[g, d - 1], b1r.at[g, d - 1], space=zpeer(d)
                )
                cp.start()
                over_z[g, d] = cp
                pending.append(cp)

    def reduce_z(g):
        with scope("reduce_z"):
            rows = pl.ds(g * 2, 2)
            total = sa[rows, z].astype(F32)
            for d in range(1, SP):
                over_z[g, d].wait_recv()
                total = total + rb1[d - 1, rows].astype(F32)
            sb1[rows] = total.astype(BF16)

    outs = []

    def output(f):
        @unrolled(D // WIDE)
        def _(n):
            at = slice(n * WIDE, (n + 1) * WIDE)
            acc = jnp.dot(ctx2[f].reshape(TM * TB, D), m2[:, at], preferred_element_type=F32)
            acc = acc + mid[f, :, at].astype(F32)
            obuf[f, :, :, at] = acc.astype(BF16).reshape(TM, TB, WIDE)

    def send_output(f):
        own = pltpu.make_async_copy(obuf.at[f, me], out_hbm.at[f, me], lsem.at[8 + f])
        own.start()
        outs.append(own)
        for d in range(1, TM):
            t = peer(d)
            cp = rcopy(obuf.at[f, t], out_hbm.at[f, me], os_.at[f, d], or_.at[f, d], tm=t)
            cp.start()
            outs.append(cp)

    merge(0)
    merge(1)
    for g in range(4):
        with scope("temporal"):
            temporal(g)
        if g == 1:
            with scope("wait_cot"):
                loads[5].wait()
                for cp in cots:
                    cp.wait_recv()
            with scope("gradient"):
                gradient(0)
        if g > 0:
            with scope("gradient"):
                gradient(g)
        if g > 1:
            reduce_core(g - 2)
    loads[4].wait()
    with scope("output0"):
        output(0)
        send_output(0)
    reduce_core(2)
    with scope("output1"):
        output(1)
        send_output(1)
    reduce_core(3)

    last = []
    for g in range(4):
        reduce_z(g)
    with scope("reduce_tm"):
        for d in range(1, TM):
            t = peer(d)
            cp = rcopy(sb1.at[t], rb2.at[d - 1], b2s.at[d], b2r.at[d], tm=t)
            cp.start()
            last.append(cp)
            pending.append(cp)
        total = sb1[me].astype(F32)
        for d in range(1, TM):
            last[d - 1].wait_recv()
            total = total + rb2[d - 1].astype(F32)
        sb2[...] = total.astype(BF16)
    with scope("reduce_batch"):
        final = []
        for i, other in enumerate(others):
            cp = rcopy(sb2, rb3.at[i], b3s.at[i], b3r.at[i], batch=other)
            cp.start()
            final.append(cp)
        for cp in final:
            cp.wait()
        wg_ref[core] = sb2[...].astype(F32) + rb3[0].astype(F32)
        wg_ref[1 - core] = rb3[1].astype(F32) + rb3[2].astype(F32)

    with scope("wait_out"):
        for cp in pending:
            cp.wait_send()
        for cp in outs:
            cp.wait()


def per_device(
    clip_tokens,
    frame_order,
    row_reach,
    spatial_gain,
    spatial_heads,
    spatial_merge,
    temporal_gain,
    temporal_heads,
    temporal_merge,
    cotangent,
):
    tokens = clip_tokens.reshape(TM, FR, TB, D).transpose(1, 0, 2, 3)
    grads = cotangent.reshape(FR, 8, TM, 4, D).transpose(2, 0, 1, 3, 4).reshape(TM, FR, TB, D)
    dma = pltpu.SemaphoreType.DMA
    vm = pltpu.VMEM
    smem = pl.BlockSpec(memory_space=pltpu.SMEM)
    vmem = pl.BlockSpec(memory_space=pltpu.VMEM)
    anym = pl.BlockSpec(memory_space=pl.ANY)
    out, wg = pl.pallas_call(
        kernel,
        out_shape=[
            jax.ShapeDtypeStruct((FR, TM, TB, D), BF16),
            jax.ShapeDtypeStruct((2, 16, D), F32),
        ],
        in_specs=[smem, smem, vmem, vmem] + [anym] * 6,
        out_specs=[anym, vmem],
        scratch_shapes=[
            vm((D, 3 * D), BF16),
            vm((D, D), BF16),
            vm((D, 3 * D), BF16),
            vm((D, D), BF16),
            vm((FR, TM, EXT, D), BF16),
            vm((TM * TB, D), BF16),
            vm((TM, TB, D), BF16),
            vm((TM, TB, D), BF16),
            vm((TM, EXT, 2 * D), BF16),
            vm((FR, 2, 384, 256), F32),
            vm((FR, TM, TB, D), BF16),
            vm((FR, TM, TB, D), BF16),
            vm((FR, TM, TB, D), BF16),
            vm((FR, TM * TB, D), BF16),
            vm((TM * TB, D), BF16),
            vm((FR, TM, TB, D), BF16),
            vm((FR, TM, TB, D), BF16),
            vm((FR, TM, TB, 2 * D), BF16),
            vm((256, 512), F32),
            vm((FR, TM, TB, D), BF16),
            vm((FR, TM, TB, D), BF16),
            vm((FR, TM, TB, D), BF16),
            vm((TM, SP, 2, 16, D), BF16),
            vm((TM, SP, 16, D), BF16),
            vm((TM, SP, 16, D), BF16),
            vm((SP - 1, TM, 16, D), BF16),
            vm((TM, 16, D), BF16),
            vm((TM - 1, 16, D), BF16),
            vm((16, D), BF16),
            vm((3, 16, D), BF16),
            dma((10,)),
            dma((FR, TM)),
            dma((FR, TM)),
            dma((FR, TM, 2)),
            dma((FR, TM, 2)),
            dma((FR, TM)),
            dma((FR, TM)),
            dma((FR, TM)),
            dma((FR, TM)),
            dma((FR, TM)),
            dma((FR, TM)),
            dma((4,)),
            dma((4,)),
            dma((4, SP - 1)),
            dma((4, SP - 1)),
            dma((TM,)),
            dma((TM,)),
            dma((3,)),
            dma((3,)),
        ],
        compiler_params=pltpu.CompilerParams(
            collective_id=0, has_side_effects=True, vmem_limit_bytes=62 * 1024 * 1024
        ),
    )(
        frame_order,
        row_reach,
        spatial_gain.reshape(1, D),
        temporal_gain.reshape(1, D),
        tokens,
        grads,
        spatial_heads,
        spatial_merge,
        temporal_heads,
        temporal_merge,
    )
    out = out.reshape(FR, TM, 8, 4, D).transpose(0, 2, 1, 3, 4).reshape(1, FR, 8, 32, D)
    return out, wg.reshape(32, D)


def solution(mesh):
    in_specs = (
        P("batch", None, "space", "tm", None),
        P("batch", None),
        P("batch", "tm"),
        P(),
        P(),
        P(),
        P(),
        P(),
        P(),
        P("batch", "tm", "space", None, None),
    )
    out_specs = (P("batch", "tm", "space", None, None), P(("tm", "space"), None))
    return jax.shard_map(
        per_device, mesh=mesh, in_specs=in_specs, out_specs=out_specs, check_vma=False
    )
```

time: 118 us -> 90.2 us (0.76)
  Pallas kernels: 108 us -> 80.1 us
    pallas_call x1, Pallas kernels: 108 us -> 80.1 us  [per_device(): pl.pallas_call(kernel, out_shape=[jax.ShapeDtypeStruct((FR, TM, TB, D), B...]
where the time goes in v2:
time: 90.2 us; the launch traced here: 90 us
  Pallas kernels  80.1 us (89%)
  local copies, waits for them, and re-layouts  9.2 us (10%)
    pallas_call x1, Pallas kernels, per_device(): pl.pallas_call(kernel, out_shape=[jax.ShapeDtypeStruct((FR, TM, TB, D), B...  80.1 us
    reshape x3, local copies, waits for them, and re-layouts, per_device(): cotangent.reshape(FR, 8, TM, 4, D).transpose(2, 0, 1, 3, 4)  3.05 us
    reshape x2, local copies, waits for them, and re-layouts, per_device(): out.reshape(FR, TM, 8, 4, D).transpose(0, 2, 1, 3, 4)  2.6 us
    reshape x2, local copies, waits for them, and re-layouts, per_device(): tokens = clip_tokens.reshape(TM, FR, TB, D).transpose(1, 0, 2, 3)  2.41 us

profile of v2, /device:TPU:1, one launch (start us, length us, event | category | flops | bytes accessed | tf_op | source)
XLA Modules:
  0.0 90.0 jit_solution(18252526712245024548)
XLA Ops:
  0.6 1.3 %reshape.30 = bf16[8,2,32,1024]{3,2,1,0:T(8,128)(2,1)S(1)} reshape(bf16[1,16,8,4,1024]{4,3,2,1,0:T(4,128)(2,1)} %param.10) | data formatting | bytes 2097152 | tf_op jit(solution)/shard_map/reshape | solution.py:528
  2.0 1.1 %copy.20 = bf16[8,2,32,1024]{3,2,0,1:T(8,128)(2,1)} copy(bf16[8,2,32,1024]{3,2,1,0:T(8,128)(2,1)S(1)} %reshape.30) | data formatting | bytes 2097152 | tf_op jit(solution)/shard_map/reshape | solution.py:528
  3.0 1.5 %reshape.31 = bf16[2,8,8,4,1024]{4,3,2,1,0:T(4,128)(2,1)S(1)} reshape(bf16[1,2,8,32,1024]{4,3,2,1,0:T(8,128)(2,1)} %param.19) | data formatting | bytes 2097152 | tf_op jit(solution)/shard_map/reshape | solution.py:529
  4.5 0.5 copy.19
  5.0 1.1 %reshape.32.cot_hbm = bf16[8,2,32,1024]{3,2,1,0:T(8,128)(2,1)} reshape(bf16[8,2,8,4,1024]{4,3,2,1,0:T(4,128)(2,1)S(1)} %bitcast.15) | data formatting | bytes 2097152 | tf_op jit(solution)/shard_map/reshape | solution.py:529
  6.1 80.1 %shard_map.113 = (bf16[2,8,32,1024]{3,2,1,0:T(8,128)(2,1)}, f32[2,16,1024]{2,1,0:T(8,128)}) custom-call(s32[1,16]{1,0:T(1,128)} %order_ref.1, s32[1,2]{1,0:T(1,128)} %reach_ref.1, f32[1,1024]{1,0:T(1,128)} %bitcast.18, f32[1,1024]{1,0:T(1,128)} %bitcast.19, bf16[2,8,32,1024]{3,2,1,0:T(8,128)(2,1)} %bitcast.14, bf16[8,2,32,1024]{3,2,1,0:T(8,128)(2,1)} %reshape.32.cot_hbm, ...), custom_call_target="tpu_custom_call" | custom-call | tf_op jit(solution)/shard_map/pallas_call | solution.py:535
  86.2 0.0 copy-start
  86.3 1.5 %reshape.33 = bf16[2,8,8,4,1024]{4,3,2,1,0:T(4,128)(2,1)S(1)} reshape(bf16[2,8,32,1024]{3,2,1,0:T(8,128)(2,1)} %get-tuple-element.4) | data formatting | bytes 2097152 | tf_op jit(solution)/shard_map/reshape | solution.py:609
  87.8 0.5 copy.16
  88.2 1.1 %reshape.34 = bf16[1,2,8,32,1024]{4,3,2,1,0:T(8,128)(2,1)} reshape(bf16[2,8,8,4,1024]{4,3,2,1,0:T(4,128)(2,1)S(1)} %copy.16) | data formatting | bytes 2097152 | tf_op jit(solution)/shard_map/reshape | solution.py:609
  89.4 0.0 copy-done
  89.4 0.7 copy.22
Async XLA Ops:
  86.2 3.1 %copy-start = (f32[2,16,1024]{2,1,0:T(8,128)S(1)}, f32[2,16,1024]{2,1,0:T(8,128)}, u32[]{:S(2)}) copy-start(f32[2,16,1024]{2,1,0:T(8,128)} %get-tuple-element.5) | copy-start | bytes 393220

commit v3 on v2

v3 whole, which is shorter than its diff:
```python
import functools
import math

import jax
import jax.numpy as jnp
from jax import lax
from jax.experimental import pallas as pl
from jax.experimental.pallas import tpu as pltpu
from jax.sharding import PartitionSpec as P

D = 1024
HEAD_DIM = 64
FLOOR = 0.5
TM = 8
SP = 4
FR = 2
TB = 32
HB = 16
EXT = TB + 2 * HB
PAIR = 128
WIDE = 1024
GROUP = 2
NEG = -1e30
QSCALE = HEAD_DIM**-0.5 * math.log2(math.e)
MESH = pl.DeviceIdType.MESH
F32 = jnp.float32
BF16 = jnp.bfloat16


def exchange_halves(a, b):
    first = iota((1, 8, 1), 1) < 4
    return jnp.where(first, a, pltpu.roll(b, 4, 1)), jnp.where(first, pltpu.roll(a, 4, 1), b)


def unrolled(count):
    def run(body):
        for n in range(count):
            body(n)

    return run


def norm_rows(values, gain):
    x = values.astype(F32).reshape(-1, D)
    x = x * lax.rsqrt(jnp.mean(x * x, axis=-1, keepdims=True) + FLOOR)
    return (x * gain).astype(BF16)


def head_masks(width):
    lane = lax.broadcasted_iota(jnp.int32, (1, width), 1)
    odd = lax.rem(lane // HEAD_DIM, 2).astype(F32)
    return (1.0 - odd) * QSCALE, odd * QSCALE


def iota(shape, dim):
    return lax.broadcasted_iota(jnp.int32, shape, dim)


def attend(chains):
    scores = [
        lax.dot_general(k, q, (((1,), (1,)), ((), ())), preferred_element_type=F32) + bias
        for q, k, _, bias in chains
    ]
    weights = []
    for s in scores:
        p = jnp.exp2(s - jnp.max(s, axis=0, keepdims=True))
        weights.append((p.astype(BF16), 1.0 / jnp.sum(p, axis=0, keepdims=True)))
    outputs = []
    for (q, _, v, _), (p, scale) in zip(chains, weights):
        count = q.shape[0] // 2
        o = lax.dot_general(v, p, (((0,), (0,)), ((), ())), preferred_element_type=F32) * scale
        both = jnp.where(iota((PAIR, count), 0) < HEAD_DIM, o[:, :count], o[:, count:])
        outputs.append(both.T.astype(BF16))
    return outputs


def kernel(
    order_ref,
    reach_ref,
    gain1_ref,
    gain2_ref,
    x_hbm,
    cot_hbm,
    w1_hbm,
    m1_hbm,
    w2_hbm,
    m2_hbm,
    out_hbm,
    wg_ref,
    w1,
    m1,
    w2,
    m2,
    xbuf,
    xn,
    qe,
    qo,
    kv,
    sbias,
    ctx,
    cbuf,
    xpos,
    mid,
    xn2,
    qe2,
    qo2,
    kv2,
    tbias,
    ctx2,
    cotraw,
    cot,
    cotin,
    obuf,
    pbuf,
    ra,
    sa,
    rb1,
    sb1,
    rb2,
    sb2,
    rb3,
    lsem,
    xs,
    xr,
    hs,
    hr,
    ts,
    tr,
    cs,
    cr,
    os_,
    or_,
    as_,
    ar,
    b1s,
    b1r,
    b2s,
    b2r,
    b3s,
    b3r,
):
    me = lax.axis_index("tm")
    z = lax.axis_index("space")
    batch = lax.axis_index("batch")
    core = lax.rem(batch, 2)
    mate = batch + 1 - 2 * core
    others = (lax.rem(batch + 2, 4), mate, lax.rem(mate + 2, 4))

    steps = ((0, 0), (0, 1), (1, 0), (3, 0), (1, 1), (3, 1), (2, 0), (2, 1))

    def peer(d, sign=1):
        dx, dy = steps[d]
        x = lax.rem(me // 2 + 4 + sign * dx, 4)
        return x * 2 + lax.rem(lax.rem(me, 2) + dy, 2)

    def zpeer(d):
        return lax.rem(z + d, SP)

    def rcopy(src, dst, send, recv, **where):
        return pltpu.make_async_remote_copy(
            src_ref=src, dst_ref=dst, send_sem=send, recv_sem=recv, device_id=where, device_id_type=MESH
        )

    def took(ref, sem):
        pltpu.make_async_copy(ref, ref, sem).wait()

    loads = [
        pltpu.make_async_copy(w1_hbm, w1, lsem.at[0]),
        pltpu.make_async_copy(x_hbm, xpos, lsem.at[1]),
        pltpu.make_async_copy(m1_hbm, m1, lsem.at[2]),
        pltpu.make_async_copy(w2_hbm, w2, lsem.at[3]),
        pltpu.make_async_copy(m2_hbm, m2, lsem.at[4]),
        pltpu.make_async_copy(cot_hbm, cotraw, lsem.at[5]),
        pltpu.make_async_copy(x_hbm.at[me, 0], xbuf.at[0, me, pl.ds(4, 8)], lsem.at[6]),
        pltpu.make_async_copy(x_hbm.at[me, 1], xbuf.at[1, me, pl.ds(4, 8)], lsem.at[7]),
    ]
    for i in (6, 7, 0, 5, 1, 2, 3, 4):
        loads[i].start()

    barrier = pltpu.get_barrier_semaphore()
    for d in range(1, TM):
        pl.semaphore_signal(barrier, inc=1, device_id={"tm": peer(d)}, device_id_type=MESH)
    for d in range(1, SP):
        pl.semaphore_signal(barrier, inc=1, device_id={"space": zpeer(d)}, device_id_type=MESH)
    for other in others:
        pl.semaphore_signal(barrier, inc=1, device_id={"batch": other}, device_id_type=MESH)
    with jax.named_scope("barrier"):
        pl.semaphore_wait(barrier, TM - 1 + SP - 1 + 3)

    sent = []

    tok = {}
    for f in range(FR):
        for d in range(1, TM):
            t = peer(d)
            tok[f, d] = rcopy(x_hbm.at[t, f], xbuf.at[f, me, pl.ds(4, 8)], xs.at[f], xr.at[f, d], tm=t)
            if f == 0:
                tok[f, d].start()
    tokens_sent = xpos.at[pl.ds(0, TM - 1), 0]

    def send_cotangent(f):
        for d in range(1, TM):
            t = peer(d)
            rcopy(cot.at[f, t], cotin.at[f, me], cs.at[f], cr.at[f], tm=t).start()
        sent.append((cot.at[f, pl.ds(0, TM - 1)], cs.at[f]))

    order_key = jnp.zeros((256, 1), jnp.int32)
    order_query = jnp.zeros((1, 512), jnp.int32)
    key_slot = iota((256, 1), 0) // 16
    query_slot = lax.rem(iota((1, 512), 1) // 16, 16)
    for f in range(FR):
        for s in range(TM):
            value = order_ref[0, s * FR + f]
            order_key = jnp.where(key_slot == f * TM + s, value, order_key)
            order_query = jnp.where(query_slot == f * TM + s, value, order_query)
    same = lax.rem(iota((256, 512), 0), 16) == lax.rem(iota((256, 512), 1), 16)
    tbias[...] = jnp.where(same & (order_key <= order_query), 0.0, NEG)
    key = iota((384, 1), 0)
    key_src = jnp.zeros((384, 1), jnp.int32)
    for n in range(1, TM):
        key_src = key_src + (key >= 48 * n).astype(jnp.int32)
    key_row = (key - 48 * key_src) // 4 - 4
    query_row = lax.rem(iota((1, 256), 1), 16) // 4
    distance = jnp.abs(key_row - query_row)
    for f in range(FR):
        for h in range(2):
            row = key_row + (z * 8 + 4 * h)
            keep = (distance <= reach_ref[0, f]) & (row >= 0) & (row < 8 * SP)
            sbias[f, h] = jnp.where(keep, 0.0, NEG)

    loads[5].wait()
    with jax.named_scope("shuffle"):
        for f in range(FR):
            for j in range(TM // 2):
                c = cotraw[f, :, 8 * j : 8 * j + 8].astype(F32).reshape(4, 2, 8, D)
                for i, block in enumerate(exchange_halves(c[:, 0], c[:, 1])):
                    cot[f, 2 * j + i] = block.reshape(TB, D).astype(BF16)
    even_mask, odd_mask = head_masks(WIDE)


    def forward(f):
        for d in range(TM):
            if d == 0:
                loads[6 + f].wait()
            else:
                if f == 0 and d == TM - 3:
                    took(tokens_sent, xs.at[0])
                    for n in range(1, TM):
                        tok[1, n].start()
                tok[f, d].wait_recv()
            s = peer(d, -1)
            above, below = zpeer(SP - 1), zpeer(1)
            rcopy(xbuf.at[f, s, pl.ds(4, 4)], xbuf.at[f, s, pl.ds(12, 4)], hs.at[f], hr.at[f], space=above).start()
            rcopy(xbuf.at[f, s, pl.ds(8, 4)], xbuf.at[f, s, pl.ds(0, 4)], hs.at[f], hr.at[f], space=below).start()
        sent.append((xbuf.at[f, :, pl.ds(4, 8)], hs.at[f]))

    def project_own(f):
        xn[...] = norm_rows(xbuf[f, :, 4:12], gain1_ref[...])

        @unrolled(D // WIDE)
        def _(n):
            at = slice(n * WIDE, (n + 1) * WIDE)
            acc = jnp.dot(xn[...], w1[:, at], preferred_element_type=F32)
            qe[:, :, at] = (acc * even_mask).astype(BF16).reshape(TM, TB, WIDE)
            qo[:, :, at] = (acc * odd_mask).astype(BF16).reshape(TM, TB, WIDE)

        @unrolled(2 * D // WIDE)
        def _(n):
            at = slice(n * WIDE, (n + 1) * WIDE)
            wat = slice(n * WIDE + D, (n + 1) * WIDE + D)
            acc = jnp.dot(xn[...], w1[:, wat], preferred_element_type=F32)
            kv[:, HB : HB + TB, at] = acc.astype(BF16).reshape(TM, TB, WIDE)

    def project_halo(f):
        took(xbuf.at[f, :, pl.ds(4, 8)], hr.at[f])
        half = TM * HB
        xn[:half] = norm_rows(xbuf[f, :, :4], gain1_ref[...])
        xn[half:] = norm_rows(xbuf[f, :, 12:], gain1_ref[...])

        @unrolled(2 * D // WIDE)
        def _(n):
            at = slice(n * WIDE, (n + 1) * WIDE)
            wat = slice(n * WIDE + D, (n + 1) * WIDE + D)
            acc = jnp.dot(xn[...], w1[:, wat], preferred_element_type=F32).astype(BF16)
            kv[:, :HB, at] = acc[:half].reshape(TM, HB, WIDE)
            kv[:, HB + TB :, at] = acc[half:].reshape(TM, HB, WIDE)

    def attend_space(f, part):
        @pl.loop(0, 4 // GROUP)
        def _(m):
            places, chains = [], []
            for u in range(GROUP):
                first_col = (m * GROUP + u) * PAIR
                to = pl.ds(pl.multiple_of(first_col, PAIR), PAIR)
                at = pl.ds(pl.multiple_of(first_col + part * 512, PAIR), PAIR)
                vat = pl.ds(pl.multiple_of(first_col + part * 512 + D, PAIR), PAIR)
                for h in range(2):
                    rows = slice(h * HB, (h + 1) * HB)
                    keys = slice(h * HB, h * HB + 3 * HB)
                    q = [ref[:, rows, at].reshape(128, PAIR) for ref in (qe, qo)]
                    k = kv[:, keys, at].reshape(384, PAIR)
                    v = kv[:, keys, vat].reshape(384, PAIR)
                    places.append((rows, to))
                    chains.append((jnp.concatenate(q, axis=0), k, v, sbias[f, h]))
            for (rows, to), both in zip(places, attend(chains)):
                ctx[f, part, :, rows, to] = both.reshape(TM, HB, PAIR)

    def send_context(f, part):
        cbuf[f, part, me] = ctx[f, part, me]
        for d in range(1, TM):
            t = peer(d)
            rcopy(ctx.at[f, part, t], cbuf.at[f, part, me], ts.at[f, part], tr.at[f, part], tm=t).start()
        if f == 0:
            sent.append((ctx.at[f, part, pl.ds(0, TM - 1)], ts.at[f, part]))

    scope = jax.named_scope
    with scope("forward0"):
        forward(0)
    send_cotangent(0)
    with scope("w1_wait"):
        loads[0].wait()
    with scope("own0"):
        project_own(0)
    with scope("halo0"):
        project_halo(0)
    with scope("attend0"):
        attend_space(0, 0)
        send_context(0, 0)
    with scope("forward1"):
        forward(1)
    with scope("attend0"):
        attend_space(0, 1)
        send_context(0, 1)
    with scope("own1"):
        project_own(1)
    with scope("halo1"):
        project_halo(1)
    with scope("attend1"):
        attend_space(1, 0)
        send_context(1, 0)
        attend_space(1, 1)
        send_context(1, 1)

    loads[1].wait()
    loads[2].wait()
    loads[3].wait()

    def merged(parts, tokens):
        joined = jnp.concatenate([parts[0], parts[1]], axis=-1).reshape(TM * TB, D)
        acc = jnp.dot(joined, m1[...], preferred_element_type=F32)
        return (acc + tokens.astype(F32).reshape(TM * TB, D)).astype(BF16)

    def merge(f):
        with scope("wait_ctx"):
            if f == 1:
                for part in range(2):
                    took(ctx.at[f, part, pl.ds(0, TM - 1)], ts.at[f, part])
                send_cotangent(1)
            for part in range(2):
                took(cbuf.at[f, part, pl.ds(0, TM - 1)], tr.at[f, part])

        with scope("merge"):
            mid[f] = merged((cbuf[f, 0], cbuf[f, 1]), xpos[:, f])
            xn2[...] = norm_rows(mid[f], gain2_ref[...])

        with scope("qkv2"):

            @unrolled(D // WIDE)
            def _(n):
                at = slice(n * WIDE, (n + 1) * WIDE)
                acc = jnp.dot(xn2[...], w2[:, at], preferred_element_type=F32)
                qe2[f, :, :, at] = (acc * even_mask).astype(BF16).reshape(TM, TB, WIDE)
                qo2[f, :, :, at] = (acc * odd_mask).astype(BF16).reshape(TM, TB, WIDE)

            @unrolled(2 * D // WIDE)
            def _(n):
                at = slice(n * WIDE, (n + 1) * WIDE)
                wat = slice(n * WIDE + D, (n + 1) * WIDE + D)
                acc = jnp.dot(xn2[...], w2[:, wat], preferred_element_type=F32)
                kv2[f, :, :, at] = acc.astype(BF16).reshape(TM, TB, WIDE)

    def temporal(g):
        places, chains = [], []
        for n in (2 * g, 2 * g + 1):
            at = slice(n * PAIR, (n + 1) * PAIR)
            vat = slice(n * PAIR + D, (n + 1) * PAIR + D)
            for b in range(2):
                rows = slice(b * 16, (b + 1) * 16)
                q = [ref[:, :, rows, at].reshape(256, PAIR) for ref in (qe2, qo2)]
                k = kv2[:, :, rows, at].reshape(256, PAIR)
                v = kv2[:, :, rows, vat].reshape(256, PAIR)
                places.append((rows, slice(n % 2 * PAIR, (n % 2 + 1) * PAIR)))
                chains.append((jnp.concatenate(q, axis=0), k, v, tbias[...]))
        for (rows, at), both in zip(places, attend(chains)):
            ctx2[g, :, :, rows, at] = both.reshape(FR, TM, 16, PAIR)

    first = []

    def gradient(g):
        a = ctx2[g].reshape(FR * TM * TB, 256)

        @unrolled(D // WIDE)
        def _(n):
            at = slice(n * WIDE, (n + 1) * WIDE)
            c = cotin[:, :, :, at].reshape(FR * TM * TB, WIDE)
            acc = lax.dot_general(a, c, (((0,), (0,)), ((), ())), preferred_element_type=F32)
            pbuf[g * 2 : g * 2 + 2, :, :, :, at] = acc.astype(BF16).reshape(2, SP, 2, 16, WIDE)

        cp = rcopy(
            pbuf.at[pl.ds(g * 2, 2), :, 1 - core], ra.at[pl.ds(g * 2, 2)], as_.at[g], ar.at[g], batch=mate
        )
        cp.start()
        first.append(cp)

    def reduce_core(g):
        with scope("reduce_core"):
            first[g].wait()
            rows = pl.ds(g * 2, 2)
            sa[rows] = (pbuf[rows, :, core].astype(F32) + ra[rows].astype(F32)).astype(BF16)
            for d in range(1, SP):
                rcopy(sa.at[rows, zpeer(d)], rb1.at[d - 1, rows], b1s.at[g], b1r.at[g], space=zpeer(d)).start()
            sent.append((sa.at[rows, pl.ds(0, SP - 1)], b1s.at[g]))

    def reduce_z(g):
        with scope("reduce_z"):
            rows = pl.ds(g * 2, 2)
            took(rb1.at[:, rows], b1r.at[g])
            total = sa[rows, z].astype(F32)
            for d in range(1, SP):
                total = total + rb1[d - 1, rows].astype(F32)
            sb1[rows] = total.astype(BF16)

    outs = []

    def output(f):
        joined = jnp.concatenate([ctx2[g, f].reshape(TM * TB, 256) for g in range(4)], axis=-1)
        acc = jnp.dot(joined, m2[...], preferred_element_type=F32) + mid[f].astype(F32)
        obuf[f] = acc.astype(BF16).reshape(TM, TB, D)
        cp = pltpu.make_async_copy(obuf.at[f, me], out_hbm.at[f, me], lsem.at[8 + f])
        cp.start()
        outs.append(cp)
        for d in range(1, TM):
            t = peer(d)
            rcopy(obuf.at[f, t], out_hbm.at[f, me], os_.at[f], or_.at[f], tm=t).start()
        sent.append((obuf.at[f, pl.ds(0, TM - 1)], os_.at[f]))
        sent.append((obuf.at[f, pl.ds(0, TM - 1)], or_.at[f]))

    merge(0)
    merge(1)
    with scope("temporal"):
        temporal(0)
        temporal(1)
    loads[4].wait()
    with scope("wait_cot"):
        for f in range(FR):
            cotin[f, me] = cot[f, me]
            took(cotin.at[f, pl.ds(0, TM - 1)], cr.at[f])
    with scope("gradient"):
        gradient(0)
        gradient(1)
    reduce_core(0)
    for g in (2, 3):
        with scope("temporal"):
            temporal(g)
        with scope("gradient"):
            gradient(g)
        reduce_core(g - 1)
    with scope("output0"):
        output(0)
    reduce_core(3)
    with scope("output1"):
        output(1)

    for g in range(4):
        reduce_z(g)
    with scope("reduce_tm"):
        for d in range(1, TM):
            t = peer(d)
            rcopy(sb1.at[t], rb2.at[d - 1], b2s, b2r, tm=t).start()
        sent.append((sb1.at[pl.ds(0, TM - 1)], b2s))
        took(rb2, b2r)
        total = sb1[me].astype(F32)
        for d in range(1, TM):
            total = total + rb2[d - 1].astype(F32)
        sb2[...] = total.astype(BF16)
    with scope("reduce_batch"):
        for i, other in enumerate(others):
            rcopy(sb2, rb3.at[i], b3s, b3r, batch=other).start()
        took(rb3, b3r)
        wg_ref[core] = sb2[...].astype(F32) + rb3[0].astype(F32)
        wg_ref[1 - core] = rb3[1].astype(F32) + rb3[2].astype(F32)

    with scope("wait_out"):
        took(rb3, b3s)
        took(tokens_sent, xs.at[1])
        for ref, sem in sent:
            took(ref, sem)
        for cp in outs:
            cp.wait()


def arrange(blocks_ref, grad_ref, out_ref, wg_ref):
    halves = []
    for j in range(2):
        a = blocks_ref[0, 2 * j].astype(F32).reshape(4, 8, D)
        b = blocks_ref[0, 2 * j + 1].astype(F32).reshape(4, 8, D)
        halves.append(exchange_halves(a, b))
    for i in range(2):
        rows = jnp.concatenate([halves[0][i], halves[1][i]], axis=1).astype(BF16)
        for r in range(4):
            out_ref[0, 2 * r + i] = rows[r]
    wg_ref[...] = grad_ref[...]


def per_device(
    clip_tokens,
    frame_order,
    row_reach,
    spatial_gain,
    spatial_heads,
    spatial_merge,
    temporal_gain,
    temporal_heads,
    temporal_merge,
    cotangent,
):
    tokens = clip_tokens.reshape(TM, FR, 8, 4, D)
    grads = cotangent.reshape(FR, 8, 32, D)
    dma = pltpu.SemaphoreType.DMA
    vm = pltpu.VMEM
    smem = pl.BlockSpec(memory_space=pltpu.SMEM)
    vmem = pl.BlockSpec(memory_space=pltpu.VMEM)
    anym = pl.BlockSpec(memory_space=pl.ANY)
    blocks, grad = pl.pallas_call(
        kernel,
        out_shape=[
            jax.ShapeDtypeStruct((FR, TM, TB, D), BF16),
            jax.ShapeDtypeStruct((2, 16, D), F32),
        ],
        in_specs=[smem, smem, vmem, vmem] + [anym] * 6,
        out_specs=[anym, vmem],
        scratch_shapes=[
            vm((D, 3 * D), BF16),
            vm((D, D), BF16),
            vm((D, 3 * D), BF16),
            vm((D, D), BF16),
            vm((FR, TM, 16, 4, D), BF16),
            vm((TM * TB, D), BF16),
            vm((TM, TB, D), BF16),
            vm((TM, TB, D), BF16),
            vm((TM, EXT, 2 * D), BF16),
            vm((FR, 2, 384, 256), F32),
            vm((FR, 2, TM, TB, 512), BF16),
            vm((FR, 2, TM, TB, 512), BF16),
            vm((TM, FR, 8, 4, D), BF16),
            vm((FR, TM * TB, D), BF16),
            vm((TM * TB, D), BF16),
            vm((FR, TM, TB, D), BF16),
            vm((FR, TM, TB, D), BF16),
            vm((FR, TM, TB, 2 * D), BF16),
            vm((256, 512), F32),
            vm((4, FR, TM, TB, 256), BF16),
            vm((FR, 8, 32, D), BF16),
            vm((FR, TM, TB, D), BF16),
            vm((FR, TM, TB, D), BF16),
            vm((FR, TM, TB, D), BF16),
            vm((TM, SP, 2, 16, D), BF16),
            vm((TM, SP, 16, D), BF16),
            vm((TM, SP, 16, D), BF16),
            vm((SP - 1, TM, 16, D), BF16),
            vm((TM, 16, D), BF16),
            vm((TM - 1, 16, D), BF16),
            vm((16, D), BF16),
            vm((3, 16, D), BF16),
            dma((10,)),
            dma((FR,)),
            dma((FR, TM)),
            dma((FR,)),
            dma((FR,)),
            dma((FR, 2)),
            dma((FR, 2)),
            dma((FR,)),
            dma((FR,)),
            dma((FR,)),
            dma((FR,)),
            dma((4,)),
            dma((4,)),
            dma((4,)),
            dma((4,)),
            dma,
            dma,
            dma,
            dma,
        ],
        compiler_params=pltpu.CompilerParams(
            collective_id=0, has_side_effects=True, vmem_limit_bytes=62 * 1024 * 1024
        ),
    )(
        frame_order,
        row_reach,
        spatial_gain.reshape(1, D),
        temporal_gain.reshape(1, D),
        tokens,
        grads,
        spatial_heads,
        spatial_merge,
        temporal_heads,
        temporal_merge,
    )
    out, wg = pl.pallas_call(
        arrange,
        grid=(FR, 2),
        out_shape=[
            jax.ShapeDtypeStruct((FR, 8, 32, D), BF16),
            jax.ShapeDtypeStruct((2, 16, D), F32),
        ],
        in_specs=[
            pl.BlockSpec((1, 4, TB, D), lambda f, k: (f, k, 0, 0)),
            pl.BlockSpec((2, 16, D), lambda f, k: (0, 0, 0)),
        ],
        out_specs=[
            pl.BlockSpec((1, 8, 16, D), lambda f, k: (f, 0, k, 0)),
            pl.BlockSpec((2, 16, D), lambda f, k: (0, 0, 0)),
        ],
    )(blocks, grad)
    return out.reshape(1, FR, 8, 32, D), wg.reshape(32, D)


def solution(mesh):
    in_specs = (
        P("batch", None, "space", "tm", None),
        P("batch", None),
        P("batch", "tm"),
        P(),
        P(),
        P(),
        P(),
        P(),
        P(),
        P("batch", "tm", "space", None, None),
    )
    out_specs = (P("batch", "tm", "space", None, None), P(("tm", "space"), None))
    return jax.shard_map(
        per_device, mesh=mesh, in_specs=in_specs, out_specs=out_specs, check_vma=False
    )
```

time: 90.2 us -> 79.9 us (0.89)
  local copies, waits for them, and re-layouts: 9.2 us -> 0 us
  Pallas kernels: 80.1 us -> 79 us
    reshape x7 -> x0, local copies, waits for them, and re-layouts: 8.07 us -> none  [the longest x3 3.05 us: per_device(): cotangent.reshape(FR, 8, TM, 4, D).transpose(2, 0, 1, 3, 4)]
    pallas_call x1, Pallas kernels: 80.1 us -> 75.5 us  [per_device(): pl.pallas_call(kernel, out_shape=[jax.ShapeDtypeStruct((FR, TM, TB, D), B...]
    pallas_call x0 -> x1, Pallas kernels: none -> 3.58 us  [per_device(): pl.pallas_call(arrange, grid=(FR, 2), out_shape=[jax.ShapeDtypeStruct((FR...]
where the time goes in v3:
time: 79.9 us; the launch traced here: 79.7 us
  Pallas kernels  79 us (99%)
    pallas_call x1, Pallas kernels, per_device(): pl.pallas_call(kernel, out_shape=[jax.ShapeDtypeStruct((FR, TM, TB, D), B...  75.5 us
    pallas_call x1, Pallas kernels, per_device(): pl.pallas_call(arrange, grid=(FR, 2), out_shape=[jax.ShapeDtypeStruct((FR...  3.58 us

profile of v3, /device:TPU:1, one launch (start us, length us, event | category | flops | bytes accessed | tf_op | source)
XLA Modules:
  0.0 79.7 jit_solution(1897797812370244895)
XLA Ops:
  0.6 75.5 %shard_map.113 = (bf16[2,8,32,1024]{3,2,1,0:T(8,128)(2,1)}, f32[2,16,1024]{2,1,0:T(8,128)}) custom-call(s32[1,16]{1,0:T(1,128)} %order_ref.1, s32[1,2]{1,0:T(1,128)} %reach_ref.1, f32[1,1024]{1,0:T(1,128)} %bitcast.8, f32[1,1024]{1,0:T(1,128)} %bitcast.9, bf16[8,2,8,4,1024]{4,3,2,1,0:T(4,128)(2,1)} %bitcast.6, bf16[2,8,32,1024]{3,2,1,0:T(8,128)(2,1)} %bitcast.7, ...), custom_call_target="tpu_custom_call" | custom-call | tf_op jit(solution)/shard_map/pallas_call | solution.py:534
  76.1 3.6 %shard_map.114 = (bf16[2,8,32,1024]{3,2,1,0:T(8,128)(2,1)}, f32[2,16,1024]{2,1,0:T(8,128)}) custom-call(bf16[2,8,32,1024]{3,2,1,0:T(8,128)(2,1)} %get-tuple-element.6.blocks_ref, f32[2,16,1024]{2,1,0:T(8,128)} %get-tuple-element.7.grad_ref), custom_call_target="tpu_custom_call" | custom-call | tf_op jit(solution)/shard_map/pallas_call | solution.py:610

commit v4 on v3

--- a/solution.py
+++ b/solution.py
@@ -237,9 +237,19 @@
                     cot[f, 2 * j + i] = block.reshape(TB, D).astype(BF16)
     even_mask, odd_mask = head_masks(WIDE)
 
-
-    def forward(f):
-        for d in range(TM):
+    has_above, has_below = z > 0, z < SP - 1
+
+    @pl.when(z == 0)
+    def _():
+        xbuf[:, :, :4] = jnp.zeros((FR, TM, 4, 4, D), BF16)
+
+    @pl.when(z == SP - 1)
+    def _():
+        xbuf[:, :, 12:] = jnp.zeros((FR, TM, 4, 4, D), BF16)
+
+
+    def forward(f, slots):
+        for d in slots:
             if d == 0:
                 loads[6 + f].wait()
             else:
@@ -249,10 +259,24 @@
                         tok[1, n].start()
                 tok[f, d].wait_recv()
             s = peer(d, -1)
-            above, below = zpeer(SP - 1), zpeer(1)
-            rcopy(xbuf.at[f, s, pl.ds(4, 4)], xbuf.at[f, s, pl.ds(12, 4)], hs.at[f], hr.at[f], space=above).start()
-            rcopy(xbuf.at[f, s, pl.ds(8, 4)], xbuf.at[f, s, pl.ds(0, 4)], hs.at[f], hr.at[f], space=below).start()
-        sent.append((xbuf.at[f, :, pl.ds(4, 8)], hs.at[f]))
+            own = xbuf.at[f, s]
+
+            @pl.when(has_above)
+            def _():
+                rcopy(own.at[pl.ds(4, 4)], own.at[pl.ds(12, 4)], hs.at[f, 0], hr.at[f, 1], space=zpeer(SP - 1)).start()
+
+            @pl.when(has_below)
+            def _():
+                rcopy(own.at[pl.ds(8, 4)], own.at[pl.ds(0, 4)], hs.at[f, 1], hr.at[f, 0], space=zpeer(1)).start()
+
+    def halo_took(f, sems):
+        @pl.when(has_above)
+        def _():
+            took(xbuf.at[f, :, pl.ds(0, 4)], sems.at[f, 0])
+
+        @pl.when(has_below)
+        def _():
+            took(xbuf.at[f, :, pl.ds(12, 4)], sems.at[f, 1])
 
     def project_own(f):
         xn[...] = norm_rows(xbuf[f, :, 4:12], gain1_ref[...])
@@ -272,7 +296,7 @@
             kv[:, HB : HB + TB, at] = acc.astype(BF16).reshape(TM, TB, WIDE)
 
     def project_halo(f):
-        took(xbuf.at[f, :, pl.ds(4, 8)], hr.at[f])
+        halo_took(f, hr)
         half = TM * HB
         xn[:half] = norm_rows(xbuf[f, :, :4], gain1_ref[...])
         xn[half:] = norm_rows(xbuf[f, :, 12:], gain1_ref[...])
@@ -315,19 +339,21 @@
 
     scope = jax.named_scope
     with scope("forward0"):
-        forward(0)
-    send_cotangent(0)
+        forward(0, range(TM))
     with scope("w1_wait"):
         loads[0].wait()
     with scope("own0"):
         project_own(0)
+        send_cotangent(0)
     with scope("halo0"):
         project_halo(0)
+    with scope("forward1"):
+        forward(1, range(6))
     with scope("attend0"):
         attend_space(0, 0)
         send_context(0, 0)
     with scope("forward1"):
-        forward(1)
+        forward(1, (6, 7))
     with scope("attend0"):
         attend_space(0, 1)
         send_context(0, 1)
@@ -439,37 +465,38 @@
         cp = pltpu.make_async_copy(obuf.at[f, me], out_hbm.at[f, me], lsem.at[8 + f])
         cp.start()
         outs.append(cp)
+
+    def send_output(f, start, count, i):
+        rows = pl.ds(start, count)
         for d in range(1, TM):
             t = peer(d)
-            rcopy(obuf.at[f, t], out_hbm.at[f, me], os_.at[f], or_.at[f], tm=t).start()
-        sent.append((obuf.at[f, pl.ds(0, TM - 1)], os_.at[f]))
-        sent.append((obuf.at[f, pl.ds(0, TM - 1)], or_.at[f]))
+            rcopy(obuf.at[f, t, rows], out_hbm.at[f, me, rows], os_.at[i], or_.at[i], tm=t).start()
+        whole = obuf.at[f, pl.ds(0, TM - 1), rows]
+        sent.append((whole, os_.at[i]))
+        sent.append((whole, or_.at[i]))
 
     merge(0)
     merge(1)
-    with scope("temporal"):
-        temporal(0)
-        temporal(1)
-    loads[4].wait()
-    with scope("wait_cot"):
-        for f in range(FR):
-            cotin[f, me] = cot[f, me]
-            took(cotin.at[f, pl.ds(0, TM - 1)], cr.at[f])
-    with scope("gradient"):
-        gradient(0)
-        gradient(1)
-    reduce_core(0)
-    for g in (2, 3):
+    for g in range(4):
         with scope("temporal"):
             temporal(g)
+        if g == 0:
+            loads[4].wait()
+            with scope("wait_cot"):
+                for f in range(FR):
+                    cotin[f, me] = cot[f, me]
+                    took(cotin.at[f, pl.ds(0, TM - 1)], cr.at[f])
+        else:
+            reduce_core(g - 1)
         with scope("gradient"):
             gradient(g)
-        reduce_core(g - 1)
     with scope("output0"):
         output(0)
+        send_output(0, 0, TB, 0)
     reduce_core(3)
     with scope("output1"):
         output(1)
+        send_output(1, 0, TB // 2, 1)
 
     for g in range(4):
         reduce_z(g)
@@ -478,6 +505,7 @@
             t = peer(d)
             rcopy(sb1.at[t], rb2.at[d - 1], b2s, b2r, tm=t).start()
         sent.append((sb1.at[pl.ds(0, TM - 1)], b2s))
+        send_output(1, TB // 2, TB // 2, 2)
         took(rb2, b2r)
         total = sb1[me].astype(F32)
         for d in range(1, TM):
@@ -493,6 +521,8 @@
     with scope("wait_out"):
         took(rb3, b3s)
         took(tokens_sent, xs.at[1])
+        halo_took(0, hs)
+        halo_took(1, hs)
         for ref, sem in sent:
             took(ref, sem)
         for cp in outs:
@@ -500,15 +530,16 @@
 
 
 def arrange(blocks_ref, grad_ref, out_ref, wg_ref):
-    halves = []
-    for j in range(2):
-        a = blocks_ref[0, 2 * j].astype(F32).reshape(4, 8, D)
-        b = blocks_ref[0, 2 * j + 1].astype(F32).reshape(4, 8, D)
-        halves.append(exchange_halves(a, b))
-    for i in range(2):
-        rows = jnp.concatenate([halves[0][i], halves[1][i]], axis=1).astype(BF16)
-        for r in range(4):
-            out_ref[0, 2 * r + i] = rows[r]
+    for k in range(2):
+        halves = []
+        for j in (2 * k, 2 * k + 1):
+            a = blocks_ref[0, 2 * j].astype(F32).reshape(4, 8, D)
+            b = blocks_ref[0, 2 * j + 1].astype(F32).reshape(4, 8, D)
+            halves.append(exchange_halves(a, b))
+        for i in range(2):
+            rows = jnp.concatenate([halves[0][i], halves[1][i]], axis=1).astype(BF16)
+            for r in range(4):
+                out_ref[0, 2 * r + i, 16 * k : 16 * k + 16] = rows[r]
     wg_ref[...] = grad_ref[...]
 
 
@@ -575,14 +606,14 @@
             dma((10,)),
             dma((FR,)),
             dma((FR, TM)),
-            dma((FR,)),
-            dma((FR,)),
+            dma((FR, 2)),
+            dma((FR, 2)),
             dma((FR, 2)),
             dma((FR, 2)),
             dma((FR,)),
             dma((FR,)),
-            dma((FR,)),
-            dma((FR,)),
+            dma((3,)),
+            dma((3,)),
             dma((4,)),
             dma((4,)),
             dma((4,)),
@@ -609,18 +640,18 @@
     )
     out, wg = pl.pallas_call(
         arrange,
-        grid=(FR, 2),
+        grid=(FR,),
         out_shape=[
             jax.ShapeDtypeStruct((FR, 8, 32, D), BF16),
             jax.ShapeDtypeStruct((2, 16, D), F32),
         ],
         in_specs=[
-            pl.BlockSpec((1, 4, TB, D), lambda f, k: (f, k, 0, 0)),
-            pl.BlockSpec((2, 16, D), lambda f, k: (0, 0, 0)),
+            pl.BlockSpec((1, TM, TB, D), lambda f: (f, 0, 0, 0)),
+            pl.BlockSpec((2, 16, D), lambda f: (0, 0, 0)),
         ],
         out_specs=[
-            pl.BlockSpec((1, 8, 16, D), lambda f, k: (f, 0, k, 0)),
-            pl.BlockSpec((2, 16, D), lambda f, k: (0, 0, 0)),
+            pl.BlockSpec((1, 8, 32, D), lambda f: (f, 0, 0, 0)),
+            pl.BlockSpec((2, 16, D), lambda f: (0, 0, 0)),
         ],
     )(blocks, grad)
     return out.reshape(1, FR, 8, 32, D), wg.reshape(32, D)

time: 79.9 us -> 76.9 us (0.962)
  Pallas kernels: 79 us -> 76.1 us
    pallas_call x1, Pallas kernels: 75.5 us -> 73.8 us  [per_device(): pl.pallas_call(kernel, out_shape=[jax.ShapeDtypeStruct((FR, TM, TB, D), B...]
    pallas_call x1, Pallas kernels: 3.58 us -> 2.24 us  [per_device(): pl.pallas_call(arrange, grid=(FR,), out_shape=[jax.ShapeDtypeStruct((FR,...]
where the time goes in v4:
time: 76.9 us; the launch traced here: 76.7 us
  Pallas kernels  76.1 us (99%)
    pallas_call x1, Pallas kernels, per_device(): pl.pallas_call(kernel, out_shape=[jax.ShapeDtypeStruct((FR, TM, TB, D), B...  73.8 us
    pallas_call x1, Pallas kernels, per_device(): pl.pallas_call(arrange, grid=(FR,), out_shape=[jax.ShapeDtypeStruct((FR,...  2.24 us

profile of v4, /device:TPU:1, one launch (start us, length us, event | category | flops | bytes accessed | tf_op | source)
XLA Modules:
  0.0 76.7 jit_solution(15551535154710072375)
XLA Ops:
  0.6 73.8 %shard_map.113 = (bf16[2,8,32,1024]{3,2,1,0:T(8,128)(2,1)}, f32[2,16,1024]{2,1,0:T(8,128)}) custom-call(s32[1,16]{1,0:T(1,128)} %order_ref.1, s32[1,2]{1,0:T(1,128)} %reach_ref.1, f32[1,1024]{1,0:T(1,128)} %bitcast.8, f32[1,1024]{1,0:T(1,128)} %bitcast.9, bf16[8,2,8,4,1024]{4,3,2,1,0:T(4,128)(2,1)} %bitcast.6, bf16[2,8,32,1024]{3,2,1,0:T(8,128)(2,1)} %bitcast.7, ...), custom_call_target="tpu_custom_call" | custom-call | tf_op jit(solution)/shard_map/pallas_call | solution.py:565
  74.5 2.2 %shard_map.114 = (bf16[2,8,32,1024]{3,2,1,0:T(8,128)(2,1)}, f32[2,16,1024]{2,1,0:T(8,128)}) custom-call(bf16[2,8,32,1024]{3,2,1,0:T(8,128)(2,1)} %get-tuple-element.6.blocks_ref, f32[2,16,1024]{2,1,0:T(8,128)} %get-tuple-element.7.grad_ref), custom_call_target="tpu_custom_call" | custom-call | tf_op jit(solution)/shard_map/pallas_call | solution.py:641
